TPU v7x, 32 devices: a 4x4x1 block of a 4x4x8 slice. The times are simulated.
32 devices in a mesh: rep: 2 (over z, core), dp: 16 (over x, y).
Axes of the slice: x: 4, y: 4, z: 1, core: 2. Of those that a mesh axis runs over, the one named last changes fastest.
The devices are a block of a 4x4x8 slice.
Arguments:
- x: bfloat16 [32, 1024, 512], P(('rep', 'dp')), parts along dimension 0
- dy: bfloat16 [32, 1024, 512], P(('rep', 'dp')), parts along dimension 0
- w_gate: bfloat16 [2, 512, 8192], P(None, 'dp')
- w_up: bfloat16 [2, 512, 8192], P(None, 'dp')
- w_down: bfloat16 [2, 8192, 512], P(None, 'dp')
- m_w_gate: float32 [2, 512, 8192], P(None, 'dp')
- m_w_up: float32 [2, 512, 8192], P(None, 'dp')
- m_w_down: float32 [2, 8192, 512], P(None, 'dp')
- v_w_gate: float32 [2, 512, 8192], P(None, 'dp')
- v_w_up: float32 [2, 512, 8192], P(None, 'dp')
- v_w_down: float32 [2, 8192, 512], P(None, 'dp')
Outputs:
- output 1: bfloat16 [4, 512, 8192], P('rep', 'dp'), parts along dimension 0
- output 2: bfloat16 [4, 512, 8192], P('rep', 'dp'), parts along dimension 0
- output 3: bfloat16 [4, 8192, 512], P('rep', 'dp'), parts along dimension 0
- output 4: float32 [4, 512, 8192], P('rep', 'dp'), parts along dimension 0
- output 5: float32 [4, 512, 8192], P('rep', 'dp'), parts along dimension 0
- output 6: float32 [4, 8192, 512], P('rep', 'dp'), parts along dimension 0
- output 7: float32 [4, 512, 8192], P('rep', 'dp'), parts along dimension 0
- output 8: float32 [4, 512, 8192], P('rep', 'dp'), parts along dimension 0
- output 9: float32 [4, 8192, 512], P('rep', 'dp'), parts along dimension 0
There are 2 independent parts. A program takes and returns all parts, laid end to end along the dimension named above; an argument that names none is the same for every part.
All inputs are finite; a program needn't handle non-finite values.
Results may differ from a plain program's by a relative error of at most 0.022.
Values are sent between devices in bfloat16 or wider.
A program may use at most 768 MiB of HBM per device.

v0:
```python
import jax
import jax.numpy as jnp
from jax import lax
from jax.sharding import PartitionSpec as P

NAMES = ("w_gate", "w_up", "w_down")


def matmul(a, w):
    return jnp.dot(a, w, preferred_element_type=jnp.float32).astype(jnp.bfloat16)


def normed(h):
    wide = h.astype(jnp.float32)
    scale = lax.rsqrt(jnp.mean(wide**2, -1, keepdims=True) + 1e-6)
    return (wide * scale).astype(jnp.bfloat16)


def layer(h, w):
    a = normed(h)
    gate = jnp.dot(a, w["w_gate"], preferred_element_type=jnp.float32)
    up = jnp.dot(a, w["w_up"], preferred_element_type=jnp.float32)
    return h + matmul((jax.nn.silu(gate) * up).astype(jnp.bfloat16), w["w_down"])


def adamw(w, m, v, g):
    m = 0.9 * m + 0.1 * g
    v = 0.95 * v + 0.05 * g * g
    step = m * lax.rsqrt(v + 1e-8) + 0.1 * w
    return (w - 0.02 * step).astype(jnp.bfloat16), m, v


def clipped(gradients, sum_of_squares, count):
    factor = jnp.minimum(1.0, 0.5 * lax.rsqrt(sum_of_squares / count + 1e-30))
    return [g * factor for g in gradients]


def solution(mesh):
    def fetched(weights, number):
        return {name: lax.all_gather(w[number], "dp", axis=0, tiled=True) for name, w in zip(NAMES, weights, strict=True)}

    def step(x, dy, *arrays):
        weights, m, v = (arrays[i : i + 3] for i in (0, 3, 6))
        layers = weights[0].shape[0]
        h, kept = x[0], []
        for number in range(layers):
            kept.append(h)
            h = layer(h, fetched(weights, number))
        by_h, mine = dy[0], [None] * layers
        for number in reversed(range(layers)):
            _, back = jax.vjp(lambda w, h: layer(h, w), fetched(weights, number), kept[number])
            by_w, by_h = back(by_h)
            mine[number] = [lax.psum_scatter(by_w[name], "dp", scatter_dimension=0, tiled=True) for name in NAMES]
        gradients = [jnp.stack([mine[number][i] for number in range(layers)]).astype(jnp.float32) for i in range(3)]
        squares = lax.psum(sum(jnp.sum(g * g) for g in gradients), "dp")
        gradients = clipped(gradients, squares, lax.psum(1, "dp") * sum(g.size for g in gradients))
        new = [adamw(w.astype(jnp.float32), m, v, g) for w, m, v, g in zip(weights, m, v, gradients, strict=True)]
        return tuple(one[which] for which in range(3) for one in new)

    states, cut = P(("rep", "dp"), None, None), P(None, "dp", None)
    return jax.shard_map(
        step,
        mesh=mesh,
        in_specs=(states, states) + (cut,) * 9,
        out_specs=(P("rep", "dp", None),) * 9,
        check_vma=False,
    )
```

profile of v0, /device:TPU:96, one launch (start us, length us, event | category | flops | bytes accessed | tf_op | source)
XLA Modules:
  0.0 1066.8 jit_solution(13146278843631236652)
XLA Ops:
  18.6 60.0 %all-gather.13.cloned.1.call-done = bf16[1,512,8192]{2,1,0:T(8,128)(2,1)} async-done(((bf16[1,32,8192]{2,1,0:T(8,128)(2,1)}), bf16[1,512,8192]{2,1,0:T(8,128)(2,1)}) %all-gather.13.cloned.1.call-update) | async-done | bytes 8388624 | tf_op jit(solution)/shard_map/all_gather | solution.py:40
  78.6 18.7 %fusion.34 = f32[1024,8192]{1,0:T(8,128)} fusion(bf16[1,512,8192]{2,1,0:T(8,128)(2,1)} %all-gather.13.cloned.1.call-done, bf16[1,1024,512]{1,2,0:T(8,128)(2,1)S(1)} %copy.20, f32[1024]{0:T(1024)S(1)} %add_rsqrt_fusion), kind=kOutput, calls=%fused_computation.45 | convolution fusion | flops 8591507456 | bytes 42995712 | tf_op jit(solution)/shard_map/dot_general | solution.py:21
  97.3 48.9 %all-gather.15.cloned.1.call-done = bf16[1,512,8192]{2,1,0:T(8,128)(2,1)} async-done(((bf16[1,32,8192]{2,1,0:T(8,128)(2,1)}), bf16[1,512,8192]{2,1,0:T(8,128)(2,1)}) %all-gather.15.cloned.1.call-update) | async-done | bytes 8388624 | tf_op jit(solution)/shard_map/all_gather | solution.py:40
  146.3 33.2 %multiply_convert_fusion.1 = (bf16[1024,8192]{1,0:T(8,128)(2,1)}, f32[1024,8192]{1,0:T(8,128)}) fusion(f32[1024,8192]{1,0:T(8,128)} %fusion.34, bf16[1,512,8192]{2,1,0:T(8,128)(2,1)} %all-gather.15.cloned.1.call-done, bf16[1,1024,512]{1,2,0:T(8,128)(2,1)S(1)} %copy.20, f32[1024]{0:T(1024)S(1)} %add_rsqrt_fusion), kind=kOutput, calls=%fused_computation.17 | convolution fusion | flops 8641839104 | bytes 93327360 | tf_op jit(solution)/shard_map/dot_general | solution.py:22
  179.5 34.5 %all-gather.17.cloned.1.call-done = bf16[1,8192,512]{2,1,0:T(8,128)(2,1)} async-done(((bf16[1,512,512]{2,1,0:T(8,128)(2,1)}), bf16[1,8192,512]{2,1,0:T(8,128)(2,1)}) %all-gather.17.cloned.1.call-update) | async-done | bytes 8388624 | tf_op jit(solution)/shard_map/all_gather | solution.py:40
  229.2 52.3 %all-gather.21.cloned.1.call-done = bf16[1,8192,512]{2,1,0:T(8,128)(2,1)} async-done(((bf16[1,512,512]{2,1,0:T(8,128)(2,1)}), bf16[1,8192,512]{2,1,0:T(8,128)(2,1)}) %all-gather.21.cloned.1.call-update) | async-done | bytes 8388624 | tf_op jit(solution)/shard_map/all_gather | solution.py:40
  296.6 52.4 %all-gather.23.cloned.1.call-done = bf16[1,512,8192]{2,1,0:T(8,128)(2,1)} async-done(((bf16[1,32,8192]{2,1,0:T(8,128)(2,1)}), bf16[1,512,8192]{2,1,0:T(8,128)(2,1)}) %all-gather.23.cloned.1.call-update) | async-done | bytes 8388624 | tf_op jit(solution)/shard_map/all_gather | solution.py:40
  349.0 18.7 %fusion.21 = f32[1024,8192]{1,0:T(8,128)} fusion(bf16[1,512,8192]{2,1,0:T(8,128)(2,1)} %all-gather.23.cloned.1.call-done, bf16[1024,512]{0,1:T(8,128)(2,1)S(1)} %get-tuple-element.27, f32[1024]{0:T(1024)S(1)} %fusion.91), kind=kOutput, calls=%fused_computation.32 | convolution fusion | flops 8591507456 | bytes 42995712 | tf_op jit(solution)/shard_map/jvp()/dot_general | solution.py:22
  367.7 48.8 %all-gather.19.cloned.1.call-done = bf16[1,512,8192]{2,1,0:T(8,128)(2,1)} async-done(((bf16[1,32,8192]{2,1,0:T(8,128)(2,1)}), bf16[1,512,8192]{2,1,0:T(8,128)(2,1)}) %all-gather.19.cloned.1.call-update) | async-done | bytes 8388624 | tf_op jit(solution)/shard_map/all_gather | solution.py:40
  416.5 41.1 %fusion.2 = (bf16[1024,8192]{1,0:T(8,128)(2,1)}, f32[1024,8192]{1,0:T(8,128)}) fusion(f32[1024,8192]{1,0:T(8,128)} %fusion.21, bf16[1024,8192]{1,0:T(8,128)(2,1)} %convolution_convert_fusion.1, bf16[1,512,8192]{2,1,0:T(8,128)(2,1)} %all-gather.19.cloned.1.call-done, bf16[1024,512]{0,1:T(8,128)(2,1)S(1)} %get-tuple-element.27, f32[1024]{0:T(1024)S(1)} %fusion.91), kind=kOutput, calls=%fused_computation.8 | convolution fusion | flops 8692170752 | bytes 110104576 | tf_op jit(solution)/shard_map/jvp()/dot_general | solution.py:21
  457.6 21.1 %fusion.71 = bf16[1024,512]{0,1:T(8,128)(2,1)S(1)} fusion(bf16[1,512,8192]{2,1,0:T(8,128)(2,1)} %all-gather.23.cloned.1.call-done, bf16[1024,8192]{1,0:T(8,128)(2,1)} %convolution_convert_fusion.1, f32[1024,8192]{1,0:T(8,128)} %get-tuple-element.29), kind=kOutput, calls=%fused_computation.99 | convolution fusion | flops 8640790528 | bytes 59768832 | tf_op jit(solution)/shard_map/transpose(jvp())/dot_general | solution.py:22
  492.4 17.4 %convolution_convert_fusion.2 = bf16[8192,512]{1,0:T(8,128)(2,1)} fusion(bf16[1024,8192]{1,0:T(8,128)(2,1)} %get-tuple-element.24, bf16[1024,512]{0,1:T(8,128)(2,1)S(1)} %fusion.80), kind=kOutput, calls=%fused_computation.30 | convolution fusion | flops 8594128896 | bytes 26214400 | tf_op jit(solution)/shard_map/transpose(jvp())/dot_general | solution.py:10
  511.0 26.8 %fusion.18 = bf16[8192,512]{1,0:T(8,128)(2,1)} fusion(f32[1024,8192]{1,0:T(8,128)} %fusion.21, bf16[1,1024,512]{2,1,0:T(8,128)(2,1)S(1)} %copy-done.18, f32[1024,8192]{1,0:T(8,128)} %get-tuple-element.29), kind=kOutput, calls=%fused_computation.27 | convolution fusion | flops 8644460544 | bytes 76546048 | tf_op jit(solution)/shard_map/transpose(jvp())/dot_general | solution.py:10
  538.0 16.1 %convolution_convert_fusion = bf16[1024,8192]{1,0:T(8,128)(2,1)} fusion(bf16[1024,512]{0,1:T(8,128)(2,1)S(1)} %fusion.80, bf16[1,8192,512]{2,1,0:T(8,128)(2,1)} %all-gather.17.cloned.1.call-done), kind=kOutput, calls=%fused_computation.24 | convolution fusion | flops 8598323200 | bytes 26214400 | tf_op jit(solution)/shard_map/transpose(jvp())/dot_general | solution.py:10
  554.0 22.3 %fusion.20 = bf16[512,8192]{1,0:T(8,128)(2,1)} fusion(bf16[1024,8192]{1,0:T(8,128)(2,1)} %convolution_convert_fusion, f32[1024,8192]{1,0:T(8,128)} %fusion.34, bf16[1,1024,512]{1,2,0:T(8,128)(2,1)S(1)} %copy-done.1, f32[1024]{0:T(1024)S(1)} %copy-done.22), kind=kOutput, calls=%fused_computation.29 | convolution fusion | flops 8646033408 | bytes 59772928 | tf_op jit(solution)/shard_map/transpose(jvp())/dot_general | solution.py:22
  577.5 22.5 %fusion.19 = bf16[512,8192]{1,0:T(8,128)(2,1)} fusion(bf16[1024,8192]{1,0:T(8,128)(2,1)} %convolution_convert_fusion.1, bf16[1024,512]{0,1:T(8,128)(2,1)S(1)} %copy-done.6, f32[1024]{0:T(1024)S(1)} %copy-done.20, f32[1024,8192]{1,0:T(8,128)} %get-tuple-element.29), kind=kOutput, calls=%fused_computation.28 | convolution fusion | flops 8646033408 | bytes 59772928 | tf_op jit(solution)/shard_map/transpose(jvp())/dot_general | solution.py:22
  600.1 32.9 %fusion.15 = bf16[512,8192]{1,0:T(8,128)(2,1)} fusion(f32[1024,8192]{1,0:T(8,128)} %fusion.34, f32[1024,8192]{1,0:T(8,128)} %get-tuple-element.25, bf16[1024,8192]{1,0:T(8,128)(2,1)} %convolution_convert_fusion, bf16[1,1024,512]{1,2,0:T(8,128)(2,1)S(1)} %copy-done.1, f32[1024]{0:T(1024)S(1)} %copy-done.22), kind=kOutput, calls=%fused_computation.26 | convolution fusion | flops 8687976448 | bytes 93327360 | tf_op jit(solution)/shard_map/transpose(jvp())/dot_general | solution.py:21
  633.2 17.1 %convolution_convert_fusion.3 = bf16[512,8192]{1,0:T(8,128)(2,1)} fusion(bf16[1024,8192]{1,0:T(8,128)(2,1)} %get-tuple-element.28, bf16[1024,512]{0,1:T(8,128)(2,1)S(1)} %copy-done.6, f32[1024]{0:T(1024)S(1)} %copy-done.20), kind=kOutput, calls=%fused_computation.31 | convolution fusion | flops 8591507456 | bytes 26218496 | tf_op jit(solution)/shard_map/transpose(jvp())/dot_general | solution.py:21
  650.4 22.5 %reduce-scatter.17.cloned.1.call-done = bf16[512,512]{1,0:T(8,128)(2,1)} async-done(((bf16[8192,512]{1,0:T(8,128)(2,1)}), bf16[512,512]{1,0:T(8,128)(2,1)}) %reduce-scatter.17.cloned.1.call-update) | async-done | bytes 524304 | tf_op jit(solution)/shard_map/reduce_scatter | solution.py:53
  675.3 80.4 %reduce-scatter.11.cloned.1.call-done = bf16[32,8192]{1,0:T(8,128)(2,1)} async-done(((bf16[512,8192]{1,0:T(8,128)(2,1)}), bf16[32,8192]{1,0:T(8,128)(2,1)}) %reduce-scatter.11.cloned.1.call-update) | async-done | bytes 524304 | tf_op jit(solution)/shard_map/reduce_scatter | solution.py:53
  755.7 82.4 %reduce-scatter.13.cloned.1.call-done = bf16[32,8192]{1,0:T(8,128)(2,1)} async-done(((bf16[512,8192]{1,0:T(8,128)(2,1)}), bf16[32,8192]{1,0:T(8,128)(2,1)}) %reduce-scatter.13.cloned.1.call-update) | async-done | bytes 524304 | tf_op jit(solution)/shard_map/reduce_scatter | solution.py:53
  840.4 80.2 %reduce-scatter.7.cloned.1.call-done = bf16[32,8192]{1,0:T(8,128)(2,1)} async-done(((bf16[512,8192]{1,0:T(8,128)(2,1)}), bf16[32,8192]{1,0:T(8,128)(2,1)}) %reduce-scatter.7.cloned.1.call-update) | async-done | bytes 524304 | tf_op jit(solution)/shard_map/reduce_scatter | solution.py:53
  920.6 82.7 %reduce-scatter.9.cloned.1.call-done = bf16[32,8192]{1,0:T(8,128)(2,1)} async-done(((bf16[512,8192]{1,0:T(8,128)(2,1)}), bf16[32,8192]{1,0:T(8,128)(2,1)}) %reduce-scatter.9.cloned.1.call-update) | async-done | bytes 524304 | tf_op jit(solution)/shard_map/reduce_scatter | solution.py:53
  1007.6 38.7 %psum.7 = f32[]{:T(128)} all-reduce(f32[]{:T(128)S(6)} %add.99), channel_id=1, replica_groups=mesh['rep'=2,'dp'=16] {'dp'}, use_global_device_ids=true, to_apply=%region_12.13 | all-reduce | flops 1 | bytes 8 | tf_op jit(solution)/shard_map/psum | solution.py:55
  (95 shorter events, 77.5 us)
Async XLA Ops:
  7.2 71.4 %all-gather.13.cloned.1.call-start = ((), (), s32[]{:S(2)}) async-start(), calls=%async_computation.12 | async-start | bytes 8912896 | tf_op jit(solution)/shard_map/all_gather | solution.py:40
  9.7 136.6 %all-gather.15.cloned.1.call-start = ((), (), s32[]{:S(2)}) async-start(), calls=%async_computation.13 | async-start | bytes 8912896 | tf_op jit(solution)/shard_map/all_gather | solution.py:40
  12.1 201.9 %all-gather.17.cloned.1.call-start = ((), (), s32[]{:S(2)}) async-start(), calls=%async_computation.14 | async-start | bytes 8912896 | tf_op jit(solution)/shard_map/all_gather | solution.py:40
  14.4 267.0 %all-gather.21.cloned.1.call-start = ((), (), s32[]{:S(2)}) async-start(), calls=%async_computation.16 | async-start | bytes 8912896 | tf_op jit(solution)/shard_map/all_gather | solution.py:40
  15.1 333.9 %all-gather.23.cloned.1.call-start = ((), (), s32[]{:S(2)}) async-start(), calls=%async_computation.17 | async-start | bytes 8912896 | tf_op jit(solution)/shard_map/all_gather | solution.py:40
  15.7 400.8 %all-gather.19.cloned.1.call-start = ((), (), s32[]{:S(2)}) async-start(), calls=%async_computation.15 | async-start | bytes 8912896 | tf_op jit(solution)/shard_map/all_gather | solution.py:40
  16.4 634.0 %reduce-scatter.15.cloned.1.call-start = ((), (), s32[]{:S(2)}) async-start(), calls=%async_computation.10 | async-start | bytes 8912896 | tf_op jit(solution)/shard_map/reduce_scatter | solution.py:53
  17.0 197.0 %copy-start = (bf16[1,1024,512]{1,2,0:T(8,128)(2,1)}, bf16[1,1024,512]{1,2,0:T(8,128)(2,1)S(1)}, u32[]{:S(2)}) copy-start(bf16[1,1024,512]{1,2,0:T(8,128)(2,1)S(1)} %copy.20) | copy-start | bytes 3145732
  17.3 129.0 %copy-start.21 = (f32[1024]{0:T(1024)}, f32[1024]{0:T(1024)S(1)}, u32[]{:S(2)}) copy-start(f32[1024]{0:T(1024)S(1)} %add_rsqrt_fusion) | copy-start | bytes 12292
  229.1 67.5 %copy-start.23 = (f32[1024]{0:T(1024)}, f32[1024]{0:T(1024)S(1)}, u32[]{:S(2)}) copy-start(f32[1024]{0:T(1024)S(1)} %get-tuple-element.26) | copy-start | bytes 12292
  229.1 262.5 %copy-start.5 = (bf16[1024,512]{0,1:T(8,128)(2,1)}, bf16[1024,512]{0,1:T(8,128)(2,1)S(1)}, u32[]{:S(2)}) copy-start(bf16[1024,512]{0,1:T(8,128)(2,1)S(1)} %get-tuple-element.27) | copy-start | bytes 3145732
  229.2 262.5 %copy-start.19 = (f32[1024]{0:T(1024)}, f32[1024]{0:T(1024)S(1)}, u32[]{:S(2)}) copy-start(f32[1024]{0:T(1024)S(1)} %fusion.91) | copy-start | bytes 12292
  457.6 21.1 %copy-start.25 = (bf16[1,512,8192]{2,1,0:T(8,128)(2,1)S(1)}, bf16[1,512,8192]{2,1,0:T(8,128)(2,1)}, u32[]{:S(2)}) copy-start(bf16[1,512,8192]{2,1,0:T(8,128)(2,1)} %all-gather.19.cloned.1.call-done) | copy-start | bytes 25165828
  478.8 12.9 %copy-start.7 = (bf16[1,1024,512]{1,2,0:T(8,128)(2,1)S(1)}, bf16[1,1024,512]{1,2,0:T(8,128)(2,1)}, u32[]{:S(2)}) copy-start(bf16[1,1024,512]{1,2,0:T(8,128)(2,1)} %copy.21) | copy-start | bytes 3145732
  509.9 163.1 %reduce-scatter.17.cloned.1.call-start = ((), (), s32[]{:S(2)}) async-start(), calls=%async_computation.11 | async-start | bytes 8912896 | tf_op jit(solution)/shard_map/reduce_scatter | solution.py:53
  537.9 16.2 %copy-start.1 = (bf16[1,1024,512]{1,2,0:T(8,128)(2,1)S(1)}, bf16[1,1024,512]{1,2,0:T(8,128)(2,1)}, u32[]{:S(2)}) copy-start(bf16[1,1024,512]{1,2,0:T(8,128)(2,1)} %copy-done) | copy-start | bytes 3145732
  537.9 16.2 %copy-start.22 = (f32[1024]{0:T(1024)S(1)}, f32[1024]{0:T(1024)}, u32[]{:S(2)}) copy-start(f32[1024]{0:T(1024)} %copy-done.21) | copy-start | bytes 12292
  537.9 217.8 %reduce-scatter.11.cloned.1.call-start = ((), (), s32[]{:S(2)}) async-start(), calls=%async_computation.8 | async-start | bytes 8912896 | tf_op jit(solution)/shard_map/reduce_scatter | solution.py:53
  576.3 261.7 %reduce-scatter.13.cloned.1.call-start = ((), (), s32[]{:S(2)}) async-start(), calls=%async_computation.9 | async-start | bytes 8912896 | tf_op jit(solution)/shard_map/reduce_scatter | solution.py:53
  600.0 320.5 %reduce-scatter.7.cloned.1.call-start = ((), (), s32[]{:S(2)}) async-start(), calls=%async_computation.6 | async-start | bytes 8912896 | tf_op jit(solution)/shard_map/reduce_scatter | solution.py:53
  633.1 370.2 %reduce-scatter.9.cloned.1.call-start = ((), (), s32[]{:S(2)}) async-start(), calls=%async_computation.7 | async-start | bytes 8912896 | tf_op jit(solution)/shard_map/reduce_scatter | solution.py:53
  650.3 396.7 %copy-start.2 = (bf16[2,512,512]{2,1,0:T(8,128)(2,1)S(1)}, bf16[2,512,512]{2,1,0:T(8,128)(2,1)}, u32[]{:S(2)}) copy-start(bf16[2,512,512]{2,1,0:T(8,128)(2,1)} %param.15) | copy-start | bytes 3145732
  650.4 402.5 %copy-start.3 = (bf16[2,32,8192]{2,1,0:T(8,128)(2,1)S(1)}, bf16[2,32,8192]{2,1,0:T(8,128)(2,1)}, u32[]{:S(2)}) copy-start(bf16[2,32,8192]{2,1,0:T(8,128)(2,1)} %param.13) | copy-start | bytes 3145732
  650.4 402.5 %copy-start.4 = (bf16[2,32,8192]{2,1,0:T(8,128)(2,1)S(1)}, bf16[2,32,8192]{2,1,0:T(8,128)(2,1)}, u32[]{:S(2)}) copy-start(bf16[2,32,8192]{2,1,0:T(8,128)(2,1)} %param.14) | copy-start | bytes 3145732
  (14 other events, 88.9 us)
Sparse Core Ops, SparseCore 0:
  10.6 67.9 all-gather.12
  81.1 65.0 all-gather.14
  148.8 65.0 all-gather.16
  216.4 65.0 all-gather.20
  283.9 65.0 all-gather.22
  351.4 65.1 all-gather.18
  510.0 79.8 reduce-scatter.14
  593.1 79.7 reduce-scatter.16
  676.2 79.4 reduce-scatter.10
  758.8 79.2 reduce-scatter.12
  841.3 79.2 reduce-scatter.6
  923.7 79.5 reduce-scatter.8
where the time goes:
time: 1070 us
  waiting for transfers between devices  647 us (60%)
  matrix products  331 us (31%)
  blocking collectives  38.7 us (4%)
  other arithmetic  19 us (2%)
  between operations  17.7 us (2%)
  local copies, waits for them, and re-layouts  12.4 us (1%)
    reduce_scatter x6, waiting for transfers between devices, step(): lax.psum_scatter(by_w[name], 'dp', scatter_dimension=0, tiled=True)  348 us
    all_gather x6, waiting for transfers between devices, fetched(): lax.all_gather(w[number], 'dp', axis=0, tiled=True)  297 us
    dot_general x5, matrix products, layer(): gate = jnp.dot(a, w['w_gate'], preferred_element_type=jnp.float32)  123 us
    dot_general x5, matrix products, layer(): up = jnp.dot(a, w['w_up'], preferred_element_type=jnp.float32)  118 us
    dot_general x5, matrix products, matmul(): jnp.dot(a, w, preferred_element_type=jnp.float32).astype(jnp.bfloat16)  90.5 us
    psum x1, blocking collectives, step(): squares = lax.psum(sum((jnp.sum(g * g) for g in gradients)), 'dp')  38.7 us
  transfers between devices with their start and end apart: 12, of which 11 were waited for; matrix products, arithmetic and copies ran while one was open for 23% of the time, Pallas kernels for 0%

commit v1 on v0

v1 whole, which is shorter than its diff:
```python
import functools
import math

import jax
import jax.numpy as jnp
from jax import lax
from jax.experimental import pallas as pl
from jax.experimental.pallas import tpu as pltpu
from jax.sharding import PartitionSpec as P

MESH = pl.DeviceIdType.MESH
BF, F32 = jnp.bfloat16, jnp.float32
LANES = 128
TILE = 512
VMEM_LIMIT = 66_000_000


def dot(a, b, over=(1, 0)):
    return lax.dot_general(a, b, (((over[0],), (over[1],)), ((), ())), preferred_element_type=F32)


def scale_of(wide):
    return lax.rsqrt(jnp.mean(wide**2, -1, keepdims=True) + 1e-6)


def adamw(w, m, v, g):
    m = 0.9 * m + 0.1 * g
    v = 0.95 * v + 0.05 * g * g
    step = m * lax.rsqrt(v + 1e-8) + 0.1 * w
    return (w - 0.02 * step).astype(BF), m, v


def clipped(gradients, sum_of_squares, count):
    factor = jnp.minimum(1.0, 0.5 * lax.rsqrt(sum_of_squares / count + 1e-30))
    return [g * factor for g in gradients]


class Torus:
    def __init__(self, n):
        me = lax.axis_index("dp")
        self.n = n
        self.at = (lax.div(me, n), lax.rem(me, n))

    def step(self, axis, by):
        return lax.rem(self.at[axis] + (by + self.n), self.n)

    def device(self, axis, by):
        x, y = self.at
        moved = self.step(axis, by)
        return {"dp": moved * self.n + y if axis == 0 else x * self.n + moved}


def greet(others):
    barrier = pltpu.get_barrier_semaphore()
    for other in others:
        pl.semaphore_signal(barrier, inc=1, device_id=other, device_id_type=MESH)
    pl.semaphore_wait(barrier, len(others))


def gather_kernel(layers, n, gu_in, d_in, gu_out, d_out, send, recv, push, pull, own):
    torus = Torus(n)
    rep = lax.axis_index("rep")
    core = lax.rem(rep, 2)
    partner = {"rep": rep + 1 - 2 * core}
    lanes, rows = gu_in.shape[-1] // 2, d_in.shape[-2]
    parts = {"all": (0, 1), "a": (0, 2), "b": (1, 2)}

    def place(k, i, j):
        first, second = torus.step(k, i), torus.step(1 - k, j)
        return (first, second) if k == 0 else (second, first)

    def refs(layer, k, block, part, mine=False, whose=core):
        which, of = parts[part]
        wide, high = lanes // of, rows // of
        cols = pl.ds(k * lanes + which * wide, wide)
        tall = pl.ds(which * high, high)
        if mine:
            return gu_in.at[layer, :, whose, :, cols], d_in.at[layer, 2 * whose + k, tall]
        x, y = block
        return gu_out.at[layer, :, x, y, whose, :, cols], d_out.at[layer, 2 * whose + k, x, y, tall]

    greet([torus.device(a, b) for a in (0, 1) for b in (1, -1)] + [partner])

    owns = []
    for layer in range(layers):
        x, y = torus.at
        owns.append(pltpu.make_async_copy(gu_in.at[layer], gu_out.at[layer, :, x, y], own.at[layer, 0]))
        owns.append(pltpu.make_async_copy(d_in.at[layer], d_out.at[layer, :, x, y], own.at[layer, 1]))
    sent = []

    def message(layer, k, group, kind, block, mine=False):
        axis = k if group == 0 else 1 - k
        part = ("all", "all", "a", "b")[kind]
        target = torus.device(axis, (1, -1)[kind % 2])
        there = refs(layer, k, block, part)
        here = refs(layer, k, block, part, mine)
        return [
            pltpu.make_async_remote_copy(s, t, send.at[layer, k, group, kind, i], recv.at[layer, k, group, kind, i], device_id=target, device_id_type=MESH)
            for i, (s, t) in enumerate(zip(here, there, strict=True))
        ]

    def out(layer, k, group, kind, block, mine=False):
        for copy in message(layer, k, group, kind, block, mine):
            copy.start()
            sent.append(copy)

    def arrived(layer, k, group, kind, block):
        for copy in message(layer, k, group, kind, block):
            copy.wait_recv()

    def swap(layer, k, number, block, theirs=False):
        whose = 1 - core if theirs else core
        both = refs(layer, k, block, "all", whose=whose)
        return [
            pltpu.make_async_remote_copy(r, r, push.at[layer, k, number, i], pull.at[layer, k, number, i], device_id=partner, device_id_type=MESH)
            for i, r in enumerate(both)
        ]

    def to_partner(layer, k, number, block):
        for copy in swap(layer, k, number, block):
            copy.start()
            sent.append(copy)

    GROUPS = ((1, 0), (2, -1), (3, 1), (4, 2))

    def first(layer):
        for group in (0, 1):
            for k in (0, 1):
                for kind in (0, 1):
                    out(layer, k, group, kind, place(k, 0, 0), mine=True)

    def second(layer):
        for kind, off, group in ((0, -1, 2), (1, 1, 3)):
            for k in (0, 1):
                block = place(k, off, 0)
                arrived(layer, k, 0, kind, block)
                out(layer, k, 0, 2 + kind, block)
                out(layer, k, group, 0, block)
                out(layer, k, group, 1, block)
                to_partner(layer, k, kind, block)

    def passed(layer, group, i):
        for kind, off in ((0, -1), (1, 1)):
            for k in (0, 1):
                block = place(k, i, off)
                arrived(layer, k, group, kind, block)
                out(layer, k, group, 2 + kind, block)
                to_partner(layer, k, 3 * group + kind, block)

    def opposite(layer):
        for k in (0, 1):
            block = place(k, 2, 0)
            arrived(layer, k, 0, 2, block)
            arrived(layer, k, 0, 3, block)
            out(layer, k, 4, 0, block)
            out(layer, k, 4, 1, block)
            to_partner(layer, k, 2, block)

    def last(layer, group, i):
        for k in (0, 1):
            block = place(k, i, 2)
            arrived(layer, k, group, 2, block)
            arrived(layer, k, group, 3, block)
            to_partner(layer, k, 3 * group + 2, block)

    def pulled(layer):
        for k in (0, 1):
            for number, (i, j) in enumerate([(-1, 0), (1, 0), (2, 0)] + [(i, j) for _, i in GROUPS for j in (-1, 1, 2)]):
                for copy in swap(layer, k, number, place(k, i, j), theirs=True):
                    copy.wait_recv()

    first(0)
    for copy in owns:
        copy.start()
    for layer in range(layers):
        second(layer)
        passed(layer, 1, 0)
        opposite(layer)
        passed(layer, 2, -1)
        passed(layer, 3, 1)
        if layer + 1 < layers:
            first(layer + 1)
        passed(layer, 4, 2)
        for group, i in GROUPS:
            last(layer, group, i)
    for layer in range(layers):
        pulled(layer)
    for copy in owns:
        copy.wait()
    for copy in sent:
        copy.wait_send()


def gather(gu, d, n):
    layers = gu.shape[0]
    any_space = pl.BlockSpec(memory_space=pl.ANY)
    dma = pltpu.SemaphoreType.DMA
    return pl.pallas_call(
        functools.partial(gather_kernel, layers, n),
        out_shape=(
            jax.ShapeDtypeStruct((layers, 2, n, n) + gu.shape[2:], BF),
            jax.ShapeDtypeStruct((layers, d.shape[1], n, n) + d.shape[2:], BF),
        ),
        in_specs=[pl.BlockSpec(memory_space=pltpu.VMEM)] * 2,
        out_specs=(any_space, any_space),
        scratch_shapes=[dma((layers, 2, 5, 4, 2)), dma((layers, 2, 5, 4, 2)), dma((layers, 2, 15, 2)), dma((layers, 2, 15, 2)), dma((layers, 2))],
        compiler_params=pltpu.CompilerParams(collective_id=0, has_side_effects=True, vmem_limit_bytes=VMEM_LIMIT),
    )(gu, d)


def forward_kernel(h_ref, gate_ref, up_ref, down_ref, out_ref, a_ref, total_ref):
    number = pl.program_id(0)

    @pl.when(number == 0)
    def _():
        wide = h_ref[...].astype(F32)
        a_ref[...] = (wide * scale_of(wide)).astype(BF)
        total_ref[...] = jnp.zeros_like(total_ref)

    half = h_ref.shape[0] // 2
    for part in range(2):
        rows = pl.ds(part * half, half)
        gate = dot(a_ref[rows, :], gate_ref[0, 0])
        up = dot(a_ref[rows, :], up_ref[0, 0])
        act = (gate * jax.nn.sigmoid(gate) * up).astype(BF)
        total_ref[rows, :] += dot(act, down_ref[0])

    @pl.when(number == pl.num_programs(0) - 1)
    def _():
        out_ref[...] = (h_ref[...].astype(F32) + total_ref[...].astype(BF).astype(F32)).astype(BF)


def forward(h, gu, down, layer):
    tokens, d = h.shape
    ff = down.shape[1]
    whole = pl.BlockSpec((tokens, d), lambda j: (0, 0))
    return pl.pallas_call(
        forward_kernel,
        grid=(ff // TILE,),
        out_shape=jax.ShapeDtypeStruct((tokens, d), BF),
        in_specs=[
            whole,
            pl.BlockSpec((1, 1, d, TILE), lambda j: (layer, 0, 0, j)),
            pl.BlockSpec((1, 1, d, TILE), lambda j: (layer, 1, 0, j)),
            pl.BlockSpec((1, TILE, d), lambda j: (layer, j, 0)),
        ],
        out_specs=whole,
        scratch_shapes=[pltpu.VMEM((tokens, d), BF), pltpu.VMEM((tokens, d), F32)],
        compiler_params=pltpu.CompilerParams(vmem_limit_bytes=VMEM_LIMIT),
        cost_estimate=pl.CostEstimate(flops=6 * tokens * d * ff, bytes_accessed=6 * d * ff, transcendentals=tokens * ff),
    )(h, gu, gu, down)


def backward_kernel(layers, n, chunks, *refs):
    hs, (dy_ref, gu_ref, down_ref, grads_ref, squares_ref) = refs[:layers], refs[layers : layers + 5]
    a_ref, at_ref, by_ref, dag_ref, dau_ref, dg_ref, du_ref, act_ref = refs[layers + 5 : layers + 13]
    gub, downb, staged, relay1, side1, partial, relay2, side2, sq_ref, sq_all, send, recv, wsem, credit, sqs, sqr = refs[layers + 13 :]
    tokens, d = dy_ref.shape
    rounds = layers * chunks
    rows, lanes = staged.shape[-2], staged.shape[-1]
    quarter = lanes // 4
    torus = Torus(n)
    ways = [(a, b) for a in (0, 1) for b in (1, -1)]

    greet([torus.device(a, b) for a, b in ways] + [torus.device(a, 2) for a in (0, 1)])

    def source(slot, k, phase, dest, half):
        if phase == 1:
            return partial.at[slot, k, :, dest, :, pl.ds(half * quarter, quarter)]
        cols = pl.ds((2 * k + half) * quarter, quarter)
        return staged.at[slot, :, dest, :, :, cols] if k == 0 else staged.at[slot, :, :, dest, :, cols]

    def message(slot, k, phase, kind, way):
        axis = k if phase == 0 else 1 - k
        relay, side = (relay1, side1) if phase == 0 else (relay2, side2)
        half = 1 - way if kind == 1 else way
        to_side = side.at[slot, k, way, half]
        if kind == 0:
            src, dst = source(slot, k, phase, torus.step(axis, 2), half), relay.at[slot, k, way]
        elif kind == 1:
            src, dst = source(slot, k, phase, torus.step(axis, 1 - 2 * way), half), to_side
        else:
            src, dst = relay.at[slot, k, way], to_side
        at = (slot, k, phase, kind, way)
        return pltpu.make_async_remote_copy(src, dst, send.at[at], recv.at[at], device_id=torus.device(axis, 1 - 2 * way), device_id_type=MESH)

    def issue(slot, phase):
        for kind in (0, 1):
            for k in (0, 1):
                for way in (0, 1):
                    message(slot, k, phase, kind, way).start()

    def middle(slot, phase):
        for k in (0, 1):
            axis = k if phase == 0 else 1 - k
            for way in (0, 1):
                message(slot, k, phase, 0, way).wait_recv()
                mine = source(slot, k, phase, torus.step(axis, 1 - 2 * way), way)
                held = (relay1 if phase == 0 else relay2).at[slot, k, way]

                def add(i, _, mine=mine, held=held):
                    at = (i,) if phase == 1 else (lax.div(i, n), lax.rem(i, n))
                    held[at] = (held[at].astype(F32) + mine[at].astype(F32)).astype(BF)
                    return 0

                lax.fori_loop(0, 3 if phase == 1 else 3 * n, add, 0)
                message(slot, k, phase, 2, way).start()

    def finish(slot, phase, layer=None, chunk=None):
        for k in (0, 1):
            axis = k if phase == 0 else 1 - k
            for way in (0, 1):
                for kind in (1, 2):
                    message(slot, k, phase, kind, way).wait_recv()
            side = (side1 if phase == 0 else side2).at[slot, k]
            for half in (0, 1):
                mine = source(slot, k, phase, torus.step(axis, 0), half)
                cols = pl.ds(half * quarter, quarter)

                def add(i, _, mine=mine, half=half, cols=cols, k=k, side=side):
                    at = (i,) if phase == 1 else (lax.div(i, n), lax.rem(i, n))
                    total = mine[at].astype(F32) + side[(0, half) + at].astype(F32) + side[(1, half) + at].astype(F32)
                    total = total.astype(BF)
                    if phase == 0:
                        partial[(slot, k) + at + (slice(None), cols)] = total
                    else:
                        grads_ref[(layer, chunk) + at + (slice(None), pl.ds((2 * k + half) * quarter, quarter))] = total
                        sq_ref[...] += total.astype(F32) ** 2
                    return 0

                lax.fori_loop(0, 3 if phase == 1 else 3 * n, add, 0)
            for way in (0, 1):
                for kind in (0, 1, 2):
                    message(slot, k, phase, kind, way).wait_send()

    def give():
        for i, (a, b) in enumerate(ways):
            pl.semaphore_signal(credit.at[i ^ 1], inc=1, device_id=torus.device(a, b), device_id_type=MESH)

    def take():
        for i in range(4):
            pl.semaphore_wait(credit.at[i], 1)

    def fetch(layer, tile, slot):
        cols = pl.ds(pl.multiple_of(tile * TILE, TILE), TILE)
        return (
            pltpu.make_async_copy(gu_ref.at[layer, :, :, cols], gub.at[slot], wsem.at[slot, 0]),
            pltpu.make_async_copy(down_ref.at[layer, cols], downb.at[slot], wsem.at[slot, 1]),
        )

    def compute(layer, slot, t, buf):
        gate_w, up_w, down_w = gub[buf, 0], gub[buf, 1], downb[buf]
        half = tokens // 2
        for part in range(2):
            these = pl.ds(part * half, half)
            gate = dot(a_ref[these, :], gate_w)
            up = dot(a_ref[these, :], up_w)
            dact = dot(by_ref[these, :], down_w, (1, 1)).astype(BF).astype(F32)
            sig = jax.nn.sigmoid(gate)
            silu = gate * sig
            act_ref[these, :] = (silu * up).astype(BF)
            du_ref[these, :] = (dact * silu).astype(BF)
            dg_ref[these, :] = (dact * up * (sig * (1.0 + gate * (1.0 - sig)))).astype(BF)
        cols = pl.ds(pl.multiple_of(t * TILE, TILE), TILE)
        staged[slot, 0, :, :, :, cols] = dot(at_ref[...], dg_ref[...]).astype(BF).reshape(n, n, rows, TILE)
        staged[slot, 1, :, :, :, cols] = dot(at_ref[...], du_ref[...]).astype(BF).reshape(n, n, rows, TILE)
        by_down = dot(act_ref[...], by_ref[...], (0, 0)).astype(BF).reshape(n, lanes // d, rows, d)
        for m in range(lanes // d):
            staged[slot, 2, t, :, :, pl.ds(m * d, d)] = by_down[:, m]
        if layer > 0:
            dag_ref[...] += dot(dg_ref[...], gate_w, (1, 1))
            dau_ref[...] += dot(du_ref[...], up_w, (1, 1))

    per = lanes // TILE
    tiles = per * chunks
    sq_ref[...] = jnp.zeros_like(sq_ref)
    by_ref[...] = dy_ref[...]
    for copy in fetch(layers - 1, 0, 0):
        copy.start()

    for layer in reversed(range(layers)):
        before = (layers - 1 - layer) * chunks
        wide = hs[layer][...].astype(F32)
        normed = wide * scale_of(wide)
        a_ref[...] = normed.astype(BF)
        at_ref[...] = normed.T.astype(BF)
        if layer > 0:
            dag_ref[...] = jnp.zeros_like(dag_ref)
            dau_ref[...] = jnp.zeros_like(dau_ref)

        def tile_step(s, _, layer=layer, before=before):
            t, r = lax.rem(s, per), before + lax.div(s, per)
            buf, slot = lax.rem(s, 2), lax.rem(r, 2)
            other = 1 - slot

            for copy in fetch(layer, s, buf):
                copy.wait()

            @pl.when(s + 1 < tiles)
            def _():
                for copy in fetch(layer, s + 1, 1 - buf):
                    copy.start()

            compute(layer, slot, t, buf)

            @pl.when((t == 0) & (r >= 1))
            def _():
                middle(other, 0)

            @pl.when((t == 1) & (r >= 2))
            def _():
                middle(slot, 1)

            @pl.when((t == 2) & (r >= 2))
            def _():
                done = r - 2
                finish(slot, 1, layers - 1 - lax.div(done, chunks), lax.rem(done, chunks))
                give()

            @pl.when(t == per - 1)
            def _():
                @pl.when(r >= 2)
                def _():
                    take()

                issue(slot, 0)

                @pl.when(r >= 1)
                def _():
                    finish(other, 0)
                    issue(other, 1)

            return 0

        lax.fori_loop(0, tiles, tile_step, 0)
        if layer > 0:
            for copy in fetch(layer - 1, 0, 0):
                copy.start()

            def norm_back(i, _, layer=layer):
                these = pl.ds(pl.multiple_of(i * LANES, LANES), LANES)
                wide = hs[layer][these, :].astype(F32)
                scale = scale_of(wide)
                da = (dag_ref[these, :].astype(BF).astype(F32) + dau_ref[these, :].astype(BF).astype(F32)).astype(BF).astype(F32)
                along = jnp.mean(da * wide, -1, keepdims=True)
                back = (da * scale - wide * (scale * scale * scale * along)).astype(BF)
                by_ref[these, :] = (by_ref[these, :].astype(F32) + back.astype(F32)).astype(BF)
                return 0

            lax.fori_loop(0, tokens // LANES, norm_back, 0)

    end = rounds - 1
    middle(end % 2, 0)
    middle((end - 1) % 2, 1)
    finish((end - 1) % 2, 1, layers - 1 - (end - 1) // chunks, (end - 1) % chunks)
    finish(end % 2, 0)
    issue(end % 2, 1)
    middle(end % 2, 1)
    finish(end % 2, 1, layers - 1 - end // chunks, end % chunks)

    mine = jnp.sum(sq_ref[...], axis=0, keepdims=True)
    mine = sum(mine[:, i * LANES : (i + 1) * LANES] for i in range(quarter // LANES))
    sq_all[0, 0] = jnp.broadcast_to(mine, sq_all.shape[2:])
    for axis in (0, 1):
        copies = [
            pltpu.make_async_remote_copy(
                sq_all.at[axis, 0], sq_all.at[axis, 1 + i], sqs.at[axis, i], sqr.at[axis, i], device_id=torus.device(axis, by), device_id_type=MESH
            )
            for i, by in enumerate((1, 2, -1))
        ]
        for copy in copies:
            copy.start()
        for copy in copies:
            copy.wait()
        total = sum(sq_all[axis, i] for i in range(1, n)) + sq_all[axis, 0]
        if axis == 0:
            sq_all[1, 0] = total
        else:
            squares_ref[...] = total


def backward(hs, dy, gu, down, n, chunks):
    layers, (tokens, d), ff = len(hs), dy.shape, down.shape[1]
    lanes = ff // chunks
    rows = d // (n * n)
    quarter = lanes // 4
    vmem, anywhere = pl.BlockSpec(memory_space=pltpu.VMEM), pl.BlockSpec(memory_space=pl.ANY)
    dma = pltpu.SemaphoreType.DMA
    return pl.pallas_call(
        functools.partial(backward_kernel, layers, n, chunks),
        out_shape=(jax.ShapeDtypeStruct((layers, chunks, 3, rows, lanes), BF), jax.ShapeDtypeStruct((8, LANES), F32)),
        in_specs=[vmem] * (layers + 1) + [anywhere] * 2,
        out_specs=(vmem, vmem),
        scratch_shapes=[
            pltpu.VMEM((tokens, d), BF),
            pltpu.VMEM((d, tokens), BF),
            pltpu.VMEM((tokens, d), BF),
            pltpu.VMEM((tokens, d), F32),
            pltpu.VMEM((tokens, d), F32),
            pltpu.VMEM((tokens, TILE), BF),
            pltpu.VMEM((tokens, TILE), BF),
            pltpu.VMEM((tokens, TILE), BF),
            pltpu.VMEM((2, 2, d, TILE), BF),
            pltpu.VMEM((2, TILE, d), BF),
            pltpu.VMEM((2, 3, n, n, rows, lanes), BF),
            pltpu.VMEM((2, 2, 2, 3, n, rows, quarter), BF),
            pltpu.VMEM((2, 2, 2, 2, 3, n, rows, quarter), BF),
            pltpu.VMEM((2, 2, 3, n, rows, 2 * quarter), BF),
            pltpu.VMEM((2, 2, 2, 3, rows, quarter), BF),
            pltpu.VMEM((2, 2, 2, 2, 3, rows, quarter), BF),
            pltpu.VMEM((rows, quarter), F32),
            pltpu.VMEM((2, n, 8, LANES), F32),
            dma((2, 2, 2, 3, 2)),
            dma((2, 2, 2, 3, 2)),
            dma((2, 2)),
            pltpu.SemaphoreType.REGULAR((4,)),
            dma((2, n - 1)),
            dma((2, n - 1)),
        ],
        compiler_params=pltpu.CompilerParams(collective_id=1, has_side_effects=True, vmem_limit_bytes=VMEM_LIMIT),
        cost_estimate=pl.CostEstimate(flops=28 * tokens * d * ff, bytes_accessed=12 * d * ff, transcendentals=2 * tokens * ff),
    )(*hs, dy, gu, down)


def solution(mesh):
    group = mesh.shape["dp"]
    n = math.isqrt(group)
    assert n == 4 and n * n == group

    def step(x, dy, *arrays):
        weights, m, v = (arrays[i : i + 3] for i in (0, 3, 6))
        layers, rows, ff = weights[0].shape
        d = weights[2].shape[-1]
        tall = ff // group
        chunks = tall // LANES
        gu = jnp.stack([w.reshape(layers, rows, group, chunks, LANES).swapaxes(2, 3).reshape(layers, rows, ff) for w in weights[:2]], axis=1)
        gu, down = gather(gu.reshape(layers, 2, 2, rows // 2, ff), weights[2].reshape(layers, chunks, LANES, d), n)
        gu, down = gu.reshape(layers, 2, d, ff), down.reshape(layers, ff, d)
        h = x[0]
        kept = [h]
        for number in range(layers - 1):
            h = forward(h, gu, down, number)
            kept.append(h)
        grads, squares = backward(kept, dy[0], gu, down, n, chunks)
        gradients = [
            grads[:, :, i].reshape(layers, chunks, rows, group, LANES).transpose(0, 2, 3, 1, 4).reshape(layers, rows, ff).astype(F32) for i in range(2)
        ]
        last = grads[:, :, 2].reshape(layers, chunks, rows, ff // chunks // d, d).swapaxes(2, 3).reshape(layers, tall, d)
        gradients.append(last.astype(F32))
        gradients = clipped(gradients, jnp.sum(squares[0]), group * sum(g.size for g in gradients))
        new = [adamw(w.astype(F32), m, v, g) for w, m, v, g in zip(weights, m, v, gradients, strict=True)]
        return tuple(one[which] for which in range(3) for one in new)

    states, cut = P(("rep", "dp"), None, None), P(None, "dp", None)
    return jax.shard_map(
        step,
        mesh=mesh,
        in_specs=(states, states) + (cut,) * 9,
        out_specs=(P("rep", "dp", None),) * 9,
        check_vma=False,
    )
```

time: 1070 us -> 550 us (0.51)
  waiting for transfers between devices: 647 us -> 0 us
  Pallas kernels: 0 us -> 503 us
  matrix products: 331 us -> 0 us
  blocking collectives: 38.7 us -> 0 us
  between operations: 17.7 us -> 1.48 us
  local copies, waits for them, and re-layouts: 12.4 us -> 26.9 us
    pallas_call x0 -> x3, Pallas kernels: none -> 503 us  [the longest x1 326 us: backward(): pl.pallas_call(functools.partial(backward_kernel, layers, n, chunks), out...]
    reduce_scatter x6 -> x0, waiting for transfers between devices: 348 us -> none  [step(): lax.psum_scatter(by_w[name], 'dp', scatter_dimension=0, tiled=True)]
    dot_general x15 -> x0, matrix products: 331 us -> none  [the longest x5 123 us: layer(): gate = jnp.dot(a, w['w_gate'], preferred_element_type=jnp.float32)]
    all_gather x6 -> x0, waiting for transfers between devices: 297 us -> none  [fetched(): lax.all_gather(w[number], 'dp', axis=0, tiled=True)]
    psum x1 -> x0, blocking collectives: 38.7 us -> none  [step(): squares = lax.psum(sum((jnp.sum(g * g) for g in gradients)), 'dp')]
    mul x0 -> x6, local copies, waits for them, and re-layouts: none -> 17.9 us  [clipped(): return [g * factor for g in gradients]]
  transfers between devices with their start and end apart: 12 -> 0, of which waited for: 11 -> 0; matrix products, arithmetic and copies ran while one was open for 23% -> 0% of each run, Pallas kernels for 0% -> 0%
where the time goes in v1:
time: 550 us; the launch traced here: 549 us
  Pallas kernels  503 us (91%)
  local copies, waits for them, and re-layouts  26.9 us (5%)
  other arithmetic  18.2 us (3%)
    pallas_call x1, Pallas kernels, backward(): pl.pallas_call(functools.partial(backward_kernel, layers, n, chunks), out...  326 us
    pallas_call x1, Pallas kernels, gather(): pl.pallas_call(functools.partial(gather_kernel, layers, n), out_shape=(ja...  144 us
    pallas_call x1, Pallas kernels, forward(): pl.pallas_call(forward_kernel, grid=(ff // TILE,), out_shape=jax.ShapeDty...  32.9 us
    mul x6, local copies, waits for them, and re-layouts, clipped(): return [g * factor for g in gradients]  17.9 us

profile of v1, /device:TPU:96, one launch (start us, length us, event | category | flops | bytes accessed | tf_op | source)
XLA Modules:
  0.0 549.2 jit_solution(7484578219195711123)
XLA Ops:
  0.6 1.8 reshape.59
  2.7 0.5 stack.7
  3.2 0.5 copy-done.3
  3.7 0.7 reshape.60
  4.7 0.5 stack.8
  5.2 1.5 pad_maximum_fusion.gu_in
  6.7 144.0 %shard_map.178 = (bf16[2,2,4,4,2,16,8192]{6,5,4,3,2,1,0:T(8,128)(2,1)}, bf16[2,4,4,4,128,512]{5,4,3,2,1,0:T(8,128)(2,1)}) custom-call(bf16[2,2,2,16,8192]{4,3,2,1,0:T(8,128)(2,1)} %pad_maximum_fusion.gu_in, bf16[2,4,128,512]{3,2,1,0:T(8,128)(2,1)} %bitcast.44), custom_call_target="tpu_custom_call" | custom-call | tf_op jit(solution)/shard_map/pallas_call | solution.py:198
  150.7 32.9 %shard_map.179.refs_1_ = bf16[1024,512]{1,0:T(8,128)(2,1)} custom-call(bf16[1024,512]{1,0:T(8,128)(2,1)} %bitcast.52, bf16[2,2,512,8192]{3,2,1,0:T(8,128)(2,1)} %bitcast.47, bf16[2,2,512,8192]{3,2,1,0:T(8,128)(2,1)} %bitcast.48, bf16[2,8192,512]{2,1,0:T(8,128)(2,1)} %bitcast.50), custom_call_target="tpu_custom_call" | custom-call | flops 25769803776 | bytes 25165824 | tf_op jit(solution)/shard_map/pallas_call | solution.py:237
  183.6 325.8 %shard_map.180 = (bf16[2,4,3,32,2048]{4,3,2,1,0:T(8,128)(2,1)}, f32[8,128]{1,0:T(8,128)}) custom-call(bf16[1024,512]{1,0:T(8,128)(2,1)} %bitcast.53, bf16[1024,512]{1,0:T(8,128)(2,1)} %shard_map.179.refs_1_, bf16[1024,512]{1,0:T(8,128)(2,1)} %bitcast.54, bf16[2,2,512,8192]{3,2,1,0:T(8,128)(2,1)} %bitcast.49, bf16[2,8192,512]{2,1,0:T(8,128)(2,1)} %bitcast.51), custom_call_target="tpu_custom_call" | custom-call | flops 120259084288 | bytes 50331648 | tf_op jit(solution)/shard_map/pallas_call | solution.py:489
  509.4 1.3 slice_reduce_fusion
  511.3 4.7 convert_multiply_fusion.3
  516.1 3.6 mul.153
  519.7 3.5 copy.24
  523.2 0.4 copy.26
  523.6 2.7 copy.23
  526.3 2.2 mul.142
  528.5 2.0 copy.25
  530.5 2.7 copy.22
  533.1 3.2 mul.130
  536.4 6.2 %fusion.8 = (bf16[2,512,512]{2,1,0:T(8,128)(2,1)}, f32[2,512,512]{2,1,0:T(8,128)}, f32[2,512,512]{2,1,0:T(8,128)}) fusion(bf16[2,512,512]{2,1,0:T(8,128)(2,1)S(1)} %copy-done.1, f32[2,4,4,32,512]{4,3,2,1,0:T(8,128)} %copy.24, f32[2,512,512]{2,1,0:T(8,128)} %param.21, f32[2,512,512]{2,1,0:T(8,128)} %param.18), kind=kLoop, calls=%fused_computation.17 | loop fusion | flops 7864320 | bytes 12582912 | tf_op jit(solution)/shard_map/convert_element_type | solution.py:30
  542.7 0.6 copy-done.6
  543.3 0.8 copy-done.7
  544.2 0.6 copy-done.8
  544.8 4.5 fusion.2
  (16 shorter events, 0.5 us)
Async XLA Ops:
  2.4 1.2 copy-start.3
  533.1 3.2 copy-start.1
  536.4 6.3 %copy-start = (f32[2,32,8192]{2,1,0:T(8,128)S(1)}, f32[2,32,8192]{2,1,0:T(8,128)}, u32[]{:S(2)}) copy-start(f32[2,32,8192]{2,1,0:T(8,128)} %mul.130) | copy-start | bytes 6291460
  536.4 6.3 %copy-start.2 = (bf16[2,32,8192]{2,1,0:T(8,128)(2,1)S(1)}, bf16[2,32,8192]{2,1,0:T(8,128)(2,1)}, u32[]{:S(2)}) copy-start(bf16[2,32,8192]{2,1,0:T(8,128)(2,1)} %param.13) | copy-start | bytes 3145732
  536.4 6.3 %copy-start.4 = (bf16[2,32,8192]{2,1,0:T(8,128)(2,1)S(1)}, bf16[2,32,8192]{2,1,0:T(8,128)(2,1)}, u32[]{:S(2)}) copy-start(bf16[2,32,8192]{2,1,0:T(8,128)(2,1)} %param.14) | copy-start | bytes 3145732
  536.4 6.3 %copy-start.5 = (f32[2,32,8192]{2,1,0:T(8,128)S(1)}, f32[2,32,8192]{2,1,0:T(8,128)}, u32[]{:S(2)}) copy-start(f32[2,32,8192]{2,1,0:T(8,128)} %param.19) | copy-start | bytes 6291460
  536.4 6.9 %copy-start.6 = (f32[2,32,8192]{2,1,0:T(8,128)S(1)}, f32[2,32,8192]{2,1,0:T(8,128)}, u32[]{:S(2)}) copy-start(f32[2,32,8192]{2,1,0:T(8,128)} %param.16) | copy-start | bytes 6291460
  536.4 7.8 %copy-start.7 = (f32[2,32,8192]{2,1,0:T(8,128)S(1)}, f32[2,32,8192]{2,1,0:T(8,128)}, u32[]{:S(2)}) copy-start(f32[2,32,8192]{2,1,0:T(8,128)} %param.20) | copy-start | bytes 6291460
  536.4 8.3 %copy-start.8 = (f32[2,32,8192]{2,1,0:T(8,128)S(1)}, f32[2,32,8192]{2,1,0:T(8,128)}, u32[]{:S(2)}) copy-start(f32[2,32,8192]{2,1,0:T(8,128)} %param.17) | copy-start | bytes 6291460

commit v2 on v0

v2 whole, which is shorter than its diff:
```python
import functools
import math

import jax
import jax.numpy as jnp
from jax import lax
from jax.experimental import pallas as pl
from jax.experimental.pallas import tpu as pltpu
from jax.sharding import PartitionSpec as P

MESH = pl.DeviceIdType.MESH
BF, F32 = jnp.bfloat16, jnp.float32
LANES = 128
TILE = 512
VMEM_LIMIT = 66_000_000
SIDES = (1, -1)


def dot(a, b, over=(1, 0)):
    return lax.dot_general(a, b, (((over[0],), (over[1],)), ((), ())), preferred_element_type=F32)


def scale_of(wide):
    return lax.rsqrt(jnp.mean(wide**2, -1, keepdims=True) + 1e-6)


def adamw(w, m, v, g):
    m = 0.9 * m + 0.1 * g
    v = 0.95 * v + 0.05 * g * g
    step = m * lax.rsqrt(v + 1e-8) + 0.1 * w
    return (w - 0.02 * step).astype(BF), m, v


class Torus:
    def __init__(self, n):
        me = lax.axis_index("dp")
        self.n = n
        self.at = (lax.div(me, n), lax.rem(me, n))

    def step(self, axis, by):
        return lax.rem(self.at[axis] + (by + self.n), self.n)

    def device(self, axis, by):
        x, y = self.at
        moved = self.step(axis, by)
        return {"dp": moved * self.n + y if axis == 0 else x * self.n + moved}


def greet(others):
    barrier = pltpu.get_barrier_semaphore()
    for other in others:
        pl.semaphore_signal(barrier, inc=1, device_id=other, device_id_type=MESH)
    pl.semaphore_wait(barrier, len(others))


def gather_kernel(layers, n, x_in, gu_in, d_in, gu_out, d_out, h_out, a_out, at_out, send, recv, push, pull, own, wsem, total_ref, gub, downb):
    torus = Torus(n)
    rep = lax.axis_index("rep")
    core = lax.rem(rep, 2)
    partner = {"rep": rep + 1 - 2 * core}
    lanes, rows = gu_in.shape[-1] // 2, d_in.shape[-2]
    tokens, d = x_in.shape
    parts = {"all": (0, 1), "a": (0, 2), "b": (1, 2)}

    def place(k, i, j):
        first, second = torus.step(k, i), torus.step(1 - k, j)
        return (first, second) if k == 0 else (second, first)

    def refs(layer, k, block, part, mine=False, whose=core):
        which, of = parts[part]
        wide, high = lanes // of, rows // of
        cols = pl.ds(k * lanes + which * wide, wide)
        tall = pl.ds(which * high, high)
        if mine:
            return gu_in.at[layer, :, whose, :, cols], d_in.at[layer, 2 * whose + k, tall]
        x, y = block
        return gu_out.at[layer, :, x, y, whose, :, cols], d_out.at[layer, 2 * whose + k, x, y, tall]

    greet([torus.device(a, b) for a in range(2) for b in SIDES] + [partner])

    def owns(layer):
        x, y = torus.at
        return (
            pltpu.make_async_copy(gu_in.at[layer], gu_out.at[layer, :, x, y], own.at[layer, 0]),
            pltpu.make_async_copy(d_in.at[layer], d_out.at[layer, :, x, y], own.at[layer, 1]),
        )

    sent = []

    def message(layer, k, group, kind, i, j):
        axis = k if group == 0 else 1 - k
        part = ("all", "all", "a", "b")[kind]
        target = torus.device(axis, SIDES[kind % 2])
        block = place(k, i, j)
        there = refs(layer, k, block, part)
        here = refs(layer, k, block, part, i == 0 and j == 0)
        return [
            pltpu.make_async_remote_copy(s, t, send.at[layer, k, group, kind, q], recv.at[layer, k, group, kind, q], device_id=target, device_id_type=MESH)
            for q, (s, t) in enumerate(zip(here, there, strict=True))
        ]

    def out(*which):
        for copy in message(*which):
            copy.start()
        sent.append((message, which))

    def arrived(*which):
        for copy in message(*which):
            copy.wait_recv()

    def swap(layer, k, number, i, j, theirs=False):
        whose = 1 - core if theirs else core
        both = refs(layer, k, place(k, i, j), "all", whose=whose)
        return [
            pltpu.make_async_remote_copy(r, r, push.at[layer, k, number, q], pull.at[layer, k, number, q], device_id=partner, device_id_type=MESH)
            for q, r in enumerate(both)
        ]

    def to_partner(*which):
        for copy in swap(*which):
            copy.start()
        sent.append((swap, which))

    GROUPS = ((1, 0), (2, -1), (3, 1), (4, 2))

    def first(layer):
        for group in range(2):
            for k in range(2):
                for kind in range(2):
                    out(layer, k, group, kind, 0, 0)

    def second(layer):
        for kind, off, group in ((0, -1, 2), (1, 1, 3)):
            for k in range(2):
                arrived(layer, k, 0, kind, off, 0)
                out(layer, k, 0, 2 + kind, off, 0)
                out(layer, k, group, 0, off, 0)
                out(layer, k, group, 1, off, 0)
                to_partner(layer, k, kind, off, 0)

    def passed(layer, group, i):
        for kind, off in ((0, -1), (1, 1)):
            for k in range(2):
                arrived(layer, k, group, kind, i, off)
                out(layer, k, group, 2 + kind, i, off)
                to_partner(layer, k, 3 * group + kind, i, off)

    def opposite(layer):
        for k in range(2):
            arrived(layer, k, 0, 2, 2, 0)
            arrived(layer, k, 0, 3, 2, 0)
            out(layer, k, 4, 0, 2, 0)
            out(layer, k, 4, 1, 2, 0)
            to_partner(layer, k, 2, 2, 0)

    def last(layer):
        for group, i in GROUPS:
            for k in range(2):
                arrived(layer, k, group, 2, i, 2)
                arrived(layer, k, group, 3, i, 2)
                to_partner(layer, k, 3 * group + 2, i, 2)

    def pulled(layer):
        for k in range(2):
            for number, (i, j) in enumerate([(-1, 0), (1, 0), (2, 0)] + [(i, j) for _, i in GROUPS for j in (-1, 1, 2)]):
                for copy in swap(layer, k, number, i, j, True):
                    copy.wait_recv()
        for copy in owns(layer):
            copy.wait()

    def stages(layer):
        def ahead():
            if layer + 1 < layers:
                first(layer + 1)
            passed(layer, 4, 2)

        return (
            lambda: second(layer),
            lambda: passed(layer, 1, 0),
            lambda: opposite(layer),
            lambda: passed(layer, 2, -1),
            lambda: passed(layer, 3, 1),
            ahead,
        )

    per = n
    tiles = d_out.shape[1] * per

    def fetch(layer, s, buf):
        cols = pl.ds(pl.multiple_of(s * TILE, TILE), TILE)
        return (
            pltpu.make_async_copy(gu_out.at[layer, :, :, :, :, :, cols], gub.at[buf], wsem.at[buf, 0]),
            pltpu.make_async_copy(d_out.at[layer, lax.div(s, per), lax.rem(s, per)], downb.at[buf], wsem.at[buf, 1]),
        )

    first(0)
    for layer in range(layers):
        for copy in owns(layer):
            copy.start()

    def enter(layer):
        wide = h_out[layer].astype(F32)
        wide = wide * scale_of(wide)
        a_out[layer] = wide.astype(BF)
        at_out[layer] = wide.T.astype(BF)

    h_out[0] = x_in[...]
    enter(0)
    for stage in stages(0):
        stage()
    last(0)
    pulled(0)

    for layer in range(layers - 1):
        todo = stages(layer + 1)
        total_ref[...] = jnp.zeros_like(total_ref)
        for copy in fetch(layer, 0, 0):
            copy.start()

        def tile_step(s, _, layer=layer, todo=todo):
            buf = lax.rem(s, 2)
            for copy in fetch(layer, s, buf):
                copy.wait()

            @pl.when(s + 1 < tiles)
            def _():
                for copy in fetch(layer, s + 1, 1 - buf):
                    copy.start()

            half = tokens // 2
            gate_w, up_w = gub[buf, 0].reshape(d, TILE), gub[buf, 1].reshape(d, TILE)
            for part in range(2):
                these = pl.ds(part * half, half)
                gate = dot(a_out[layer, these, :], gate_w)
                up = dot(a_out[layer, these, :], up_w)
                act = (gate * jax.nn.sigmoid(gate) * up).astype(BF)
                total_ref[these, :] += dot(act, downb[buf].reshape(TILE, d))

            for number, stage in enumerate(todo):
                pl.when(s == 2 * number + 1)(stage)
            return 0

        lax.fori_loop(0, tiles, tile_step, 0)
        h_out[layer + 1] = (h_out[layer].astype(F32) + total_ref[...].astype(BF).astype(F32)).astype(BF)
        enter(layer + 1)
        last(layer + 1)
        pulled(layer + 1)

    for make, which in sent:
        for copy in make(*which):
            copy.wait_send()


def gather(x, gu, d, n):
    layers, (tokens, wide) = gu.shape[0], x.shape
    anywhere, vmem = pl.BlockSpec(memory_space=pl.ANY), pl.BlockSpec(memory_space=pltpu.VMEM)
    dma = pltpu.SemaphoreType.DMA
    return pl.pallas_call(
        functools.partial(gather_kernel, layers, n),
        out_shape=(
            jax.ShapeDtypeStruct((layers, 2, n, n) + gu.shape[2:], BF),
            jax.ShapeDtypeStruct((layers, d.shape[1], n, n) + d.shape[2:], BF),
            jax.ShapeDtypeStruct((layers, tokens, wide), BF),
            jax.ShapeDtypeStruct((layers, tokens, wide), BF),
            jax.ShapeDtypeStruct((layers, wide, tokens), BF),
        ),
        in_specs=[vmem] * 3,
        out_specs=(anywhere, anywhere, vmem, vmem, vmem),
        scratch_shapes=[
            dma((layers, 2, 5, 4, 2)),
            dma((layers, 2, 5, 4, 2)),
            dma((layers, 2, 15, 2)),
            dma((layers, 2, 15, 2)),
            dma((layers, 2)),
            dma((2, 2)),
            pltpu.VMEM((tokens, wide), F32),
            pltpu.VMEM((2, 2, n, n) + gu.shape[2:-1] + (TILE,), BF),
            pltpu.VMEM((2, n) + d.shape[2:], BF),
        ],
        compiler_params=pltpu.CompilerParams(collective_id=0, has_side_effects=True, vmem_limit_bytes=VMEM_LIMIT),
    )(x, gu, d)


class Stream:
    def __init__(self, torus, slots, refs, result):
        self.torus, self.slots, self.result = torus, slots, result
        self.staged, relay1, side1, self.partial, relay2, side2, self.send, self.recv, self.credit = refs
        self.relay, self.side = (relay1, relay2), (side1, side2)
        self.quarter = self.staged.shape[-1] // 4

    def slot(self, r):
        return lax.rem(r, self.slots)

    def source(self, slot, k, phase, dest, half):
        q = self.quarter
        if phase == 1:
            return self.partial.at[slot, k, :, dest, :, pl.ds(half * q, q)]
        cols = pl.ds((2 * k + half) * q, q)
        return self.staged.at[slot, :, dest, :, :, cols] if k == 0 else self.staged.at[slot, :, :, dest, :, cols]

    def message(self, slot, k, phase, kind, way):
        torus = self.torus
        axis = k if phase == 0 else 1 - k
        half = 1 - way if kind == 1 else way
        held, to_side = self.relay[phase].at[slot, k, way], self.side[phase].at[slot, k, way, half]
        if kind == 0:
            src, dst = self.source(slot, k, phase, torus.step(axis, 2), half), held
        elif kind == 1:
            src, dst = self.source(slot, k, phase, torus.step(axis, SIDES[way]), half), to_side
        else:
            src, dst = held, to_side
        at = (slot, k, phase, kind, way)
        target = torus.device(axis, SIDES[way])
        return pltpu.make_async_remote_copy(src, dst, self.send.at[at], self.recv.at[at], device_id=target, device_id_type=MESH)

    def issue(self, r, phase):
        for kind in range(2):
            for k in range(2):
                for way in range(2):
                    self.message(self.slot(r), k, phase, kind, way).start()

    def middle(self, r, phase):
        slot = self.slot(r)
        for k in range(2):
            axis = k if phase == 0 else 1 - k
            for way in range(2):
                self.message(slot, k, phase, 0, way).wait_recv()
                mine = self.source(slot, k, phase, self.torus.step(axis, SIDES[way]), way)
                held = self.relay[phase].at[slot, k, way]
                held[...] = (held[...].astype(F32) + mine[...].astype(F32)).astype(BF)
                self.message(slot, k, phase, 2, way).start()

    def finish(self, r, phase):
        slot, q = self.slot(r), self.quarter
        for k in range(2):
            axis = k if phase == 0 else 1 - k
            for way in range(2):
                for kind in (1, 2):
                    self.message(slot, k, phase, kind, way).wait_recv()
            for half in range(2):
                mine = self.source(slot, k, phase, self.torus.step(axis, 0), half)
                side = self.side[phase]
                total = mine[...].astype(F32) + side[slot, k, 0, half].astype(F32) + side[slot, k, 1, half].astype(F32)
                if phase == 0:
                    self.partial[slot, k, :, :, :, pl.ds(half * q, q)] = total.astype(BF)
                else:
                    self.result(r, pl.ds((2 * k + half) * q, q), total.astype(BF))
            for way in range(2):
                for kind in (0, 1, 2):
                    self.message(slot, k, phase, kind, way).wait_send()

    def ways(self):
        return [(i, self.torus.device(a, b)) for i, (a, b) in enumerate((axis, side) for axis in range(2) for side in SIDES)]

    def give(self):
        for i, device in self.ways():
            pl.semaphore_signal(self.credit.at[i ^ 1], inc=1, device_id=device, device_id_type=MESH)

    def take(self):
        for i in range(4):
            pl.semaphore_wait(self.credit.at[i], 1)


LAG = 2
SLOTS = 5 * LAG


def backward_kernel(layers, n, *refs):
    hs_ref, a_ref, at_ref, dy_ref, gu_ref, down_ref, grads_ref, down_grads_ref, squares_ref, by_ref, dag_ref, dau_ref, dg_ref, du_ref, act_ref = refs[:15]
    gub, downb, wsem, sq_ref, sq_all, sqs, sqr, *stream = refs[15:]
    tokens, d = dy_ref.shape
    tiles, rows = grads_ref.shape[1], grads_ref.shape[3]
    per = n
    pairs = down_grads_ref.shape[2] // 2
    chunks, total_tiles = tiles // per, layers * tiles
    turns = per + pairs
    rounds = layers * chunks * turns
    torus = Torus(n)

    greet([torus.device(a, b) for a in range(2) for b in SIDES] + [torus.device(a, 2) for a in range(2)])

    def store(r, cols, total):
        chunk, turn = lax.div(r, turns), lax.rem(r, turns)
        layer, chunk = layers - 1 - lax.div(chunk, chunks), lax.rem(chunk, chunks)

        @pl.when(turn < per)
        def _():
            grads_ref[layer, chunk * per + turn, :, :, cols] = total

        @pl.when(turn >= per)
        def _():
            down_grads_ref[layer, chunk, pl.ds(2 * (turn - per), 2), :, cols] = total

        wide = total.astype(F32)
        sq_ref[...] += jnp.sum(wide * wide, axis=0)

    sums = Stream(torus, SLOTS, stream, store)

    def fetch(r, buf):
        layer, tile = layers - 1 - lax.div(r, tiles), lax.rem(r, tiles)
        cols = pl.ds(pl.multiple_of(tile * TILE, TILE), TILE)
        return (
            pltpu.make_async_copy(gu_ref.at[layer, :, :, cols], gub.at[buf], wsem.at[buf, 0]),
            pltpu.make_async_copy(down_ref.at[layer, cols], downb.at[buf], wsem.at[buf, 1]),
        )

    def norm_back(layer):
        def block(i, _):
            these = pl.ds(pl.multiple_of(i * LANES, LANES), LANES)
            wide = hs_ref[layer, these, :].astype(F32)
            scale = scale_of(wide)
            da = (dag_ref[these, :].astype(BF).astype(F32) + dau_ref[these, :].astype(BF).astype(F32)).astype(BF).astype(F32)
            along = jnp.mean(da * wide, -1, keepdims=True)
            back = (da * scale - wide * (scale * scale * scale * along)).astype(BF)
            by_ref[these, :] = (by_ref[these, :].astype(F32) + back.astype(F32)).astype(BF)
            return 0

        lax.fori_loop(0, tokens // LANES, block, 0)

    def compute(r, layer):
        buf, t = lax.rem(r, 2), lax.rem(r, per)
        first = lax.div(r, per) * turns
        gate_w, up_w, down_w = gub[buf, 0], gub[buf, 1], downb[buf]
        half = tokens // 2
        for part in range(2):
            these = pl.ds(part * half, half)
            gate = dot(a_ref[layer, these, :], gate_w)
            up = dot(a_ref[layer, these, :], up_w)
            dact = dot(by_ref[these, :], down_w, (1, 1)).astype(BF).astype(F32)
            sig = jax.nn.sigmoid(gate)
            silu = gate * sig
            act_ref[these, :] = (silu * up).astype(BF)
            du_ref[these, :] = (dact * silu).astype(BF)
            dg_ref[these, :] = (dact * up * (sig * (1.0 + gate * (1.0 - sig)))).astype(BF)
        for which, ref in enumerate((dg_ref, du_ref)):
            sums.staged[sums.slot(first + t), which] = dot(at_ref[layer], ref[...]).astype(BF).reshape(n, n, rows, TILE)
        by_down = dot(act_ref[...], by_ref[...], (0, 0)).astype(BF).reshape(n, 2 * pairs, rows, d)
        for m in range(2 * pairs):
            sums.staged[sums.slot(first + per + m // 2), m % 2, t] = by_down[:, m]

        @pl.when(layer > 0)
        def _():
            dag_ref[...] += dot(dg_ref[...], gate_w, (1, 1))
            dau_ref[...] += dot(du_ref[...], up_w, (1, 1))

    def turn(r, _):
        @pl.when(r < rounds)
        def _():
            @pl.when(r >= SLOTS)
            def _():
                sums.take()

            sums.issue(r, 0)

        def late(stages):
            return (r >= stages * LAG) & (r < rounds + stages * LAG)

        @pl.when(late(1))
        def _():
            sums.middle(r - LAG, 0)

        @pl.when(late(2))
        def _():
            sums.finish(r - 2 * LAG, 0)
            sums.issue(r - 2 * LAG, 1)

        @pl.when(late(3))
        def _():
            sums.middle(r - 3 * LAG, 1)

        @pl.when(late(4))
        def _():
            sums.finish(r - 4 * LAG, 1)

            @pl.when(r - 4 * LAG + SLOTS < rounds)
            def _():
                sums.give()

        return 0

    sq_ref[...] = jnp.zeros_like(sq_ref)
    by_ref[...] = dy_ref[...]
    for copy in fetch(0, 0):
        copy.start()

    def tile_step(r, _):
        t, first = lax.rem(r, per), lax.div(r, per) * turns

        @pl.when(r < total_tiles)
        def _():
            layer = layers - 1 - lax.div(r, tiles)
            for copy in fetch(r, lax.rem(r, 2)):
                copy.wait()

            @pl.when(r + 1 < total_tiles)
            def _():
                for copy in fetch(r + 1, 1 - lax.rem(r, 2)):
                    copy.start()

            @pl.when(lax.rem(r, tiles) == 0)
            def _():
                @pl.when(r > 0)
                def _():
                    norm_back(layer + 1)

                dag_ref[...] = jnp.zeros_like(dag_ref)
                dau_ref[...] = jnp.zeros_like(dau_ref)

            compute(r, layer)

        more = 1 + pairs * lax.div(t + 1, per) + (4 * LAG - 1) * lax.div(r, total_tiles)
        lax.fori_loop(first + t, first + t + more, turn, 0)
        return 0

    lax.fori_loop(0, total_tiles + 1, tile_step, 0)

    mine = jnp.sum(sq_ref[...], axis=0, keepdims=True)
    sq_all[0, 0] = jnp.broadcast_to(mine, sq_all.shape[2:])
    for axis in range(2):
        copies = [
            pltpu.make_async_remote_copy(
                sq_all.at[axis, 0], sq_all.at[axis, 1 + i], sqs.at[axis, i], sqr.at[axis, i], device_id=torus.device(axis, by), device_id_type=MESH
            )
            for i, by in enumerate((1, 2, -1))
        ]
        for copy in copies:
            copy.start()
        for copy in copies:
            copy.wait()
        total = sum(sq_all[axis, i] for i in range(1, n)) + sq_all[axis, 0]
        if axis == 0:
            sq_all[1, 0] = total
        else:
            squares_ref[...] = total


def backward(hs, normed, turned, dy, gu, down, n):
    layers, (tokens, d), ff = hs.shape[0], dy.shape, down.shape[1]
    rows, quarter, tiles = d // (n * n), TILE // 4, ff // TILE
    vmem, anywhere = pl.BlockSpec(memory_space=pltpu.VMEM), pl.BlockSpec(memory_space=pl.ANY)
    dma = pltpu.SemaphoreType.DMA

    both, block = (SLOTS, 2, 2), (2, n, rows, quarter)
    stream = [
        pltpu.VMEM((SLOTS, 2, n, n, rows, TILE), BF),
        pltpu.VMEM(both + block, BF),
        pltpu.VMEM(both + (2,) + block, BF),
        pltpu.VMEM((SLOTS, 2, 2, n, rows, 2 * quarter), BF),
        pltpu.VMEM(both + (2, rows, quarter), BF),
        pltpu.VMEM(both + (2, 2, rows, quarter), BF),
        dma(both + (3, 2)),
        dma(both + (3, 2)),
        pltpu.SemaphoreType.REGULAR((4,)),
    ]

    return pl.pallas_call(
        functools.partial(backward_kernel, layers, n),
        out_shape=(
            jax.ShapeDtypeStruct((layers, tiles, 2, rows, TILE), BF),
            jax.ShapeDtypeStruct((layers, tiles // n, LANES // rows, rows, d), BF),
            jax.ShapeDtypeStruct((8, LANES), F32),
        ),
        in_specs=[vmem] * 4 + [anywhere] * 2,
        out_specs=(vmem, vmem, vmem),
        scratch_shapes=[
            pltpu.VMEM((tokens, d), BF),
            pltpu.VMEM((tokens, d), F32),
            pltpu.VMEM((tokens, d), F32),
            pltpu.VMEM((tokens, TILE), BF),
            pltpu.VMEM((tokens, TILE), BF),
            pltpu.VMEM((tokens, TILE), BF),
            pltpu.VMEM((2, 2, d, TILE), BF),
            pltpu.VMEM((2, TILE, d), BF),
            dma((2, 2)),
            pltpu.VMEM((rows, quarter), F32),
            pltpu.VMEM((2, n, 8, LANES), F32),
            dma((2, n - 1)),
            dma((2, n - 1)),
        ]
        + stream,
        compiler_params=pltpu.CompilerParams(collective_id=1, has_side_effects=True, vmem_limit_bytes=VMEM_LIMIT),
        cost_estimate=pl.CostEstimate(flops=28 * tokens * d * ff, bytes_accessed=12 * d * ff, transcendentals=2 * tokens * ff),
    )(hs, normed, turned, dy, gu, down)


def update_kernel(count, n, grads_ref, down_grads_ref, squares_ref, *refs):
    w, m, v, new_w, new_m, new_v = (refs[i : i + 3] for i in range(0, 18, 3))
    squares = jnp.sum(squares_ref[0:1, :], axis=1, keepdims=True)
    factor = jnp.minimum(1.0, 0.5 * lax.rsqrt(squares / count + 1e-30))

    def put(which, at, g):
        new = adamw(w[which][at].astype(F32), m[which][at], v[which][at], g.astype(F32) * factor)
        for ref, value in zip((new_w[which], new_m[which], new_v[which]), new, strict=True):
            ref[at] = value

    t = pl.program_id(1)
    rows, span = w[0].shape[1:]
    for which in range(2):
        for y in range(n):
            for q in range(span // (n * LANES)):
                at = (0, slice(None), pl.ds((y * (span // (n * LANES)) + q) * LANES, LANES))
                put(which, at, grads_ref[0, q * n + t, which, :, pl.ds(y * LANES, LANES)])
    for i in range(down_grads_ref.shape[2]):
        put(2, (0, pl.ds(i * rows, rows)), down_grads_ref[0, 0, i])


def update(grads, down_grads, squares, weights, m, v, n, count):
    layers, rows, ff = weights[0].shape
    tall, d = weights[2].shape[1:]
    steps = n
    wide = pl.BlockSpec((1, rows, ff // steps), lambda l, t: (l, 0, t))
    high = pl.BlockSpec((1, tall // steps, d), lambda l, t: (l, t, 0))
    three = [wide, wide, high]
    shapes = [jax.ShapeDtypeStruct(w.shape, kind) for kind in (BF, F32, F32) for w in weights]
    return pl.pallas_call(
        functools.partial(update_kernel, count, n),
        grid=(layers, steps),
        out_shape=tuple(shapes),
        in_specs=[
            pl.BlockSpec((1,) + grads.shape[1:], lambda l, t: (l, 0, 0, 0, 0)),
            pl.BlockSpec((1, 1) + down_grads.shape[2:], lambda l, t: (l, t, 0, 0, 0)),
            pl.BlockSpec(squares.shape, lambda l, t: (0, 0)),
        ]
        + three * 3,
        out_specs=tuple(three * 3),
        compiler_params=pltpu.CompilerParams(vmem_limit_bytes=VMEM_LIMIT),
    )(grads, down_grads, squares, *weights, *m, *v)


def solution(mesh):
    group = mesh.shape["dp"]
    n = math.isqrt(group)
    assert n == 4 and n * n == group

    def step(x, dy, *arrays):
        weights, m, v = (arrays[i : i + 3] for i in (0, 3, 6))
        layers, rows, ff = weights[0].shape
        d = weights[2].shape[-1]
        tall = ff // group
        chunks = tall // LANES
        gu = jnp.stack([w.reshape(layers, rows, group, chunks, LANES).swapaxes(2, 3).reshape(layers, rows, ff) for w in weights[:2]], axis=1)
        gu, down, *states = gather(x[0], gu.reshape(layers, 2, 2, rows // 2, ff), weights[2].reshape(layers, chunks, LANES, d), n)
        gu, down = gu.reshape(layers, 2, d, ff), down.reshape(layers, ff, d)
        grads, down_grads, squares = backward(*states, dy[0], gu, down, n)
        return update(grads, down_grads, squares, weights, m, v, n, group * sum(w.size for w in weights))

    states, cut = P(("rep", "dp"), None, None), P(None, "dp", None)
    return jax.shard_map(
        step,
        mesh=mesh,
        in_specs=(states, states) + (cut,) * 9,
        out_specs=(P("rep", "dp", None),) * 9,
        check_vma=False,
    )
```

time: 1070 us -> 468 us (0.44)
  waiting for transfers between devices: 647 us -> 0 us
  Pallas kernels: 0 us -> 461 us
  matrix products: 331 us -> 0 us
  blocking collectives: 38.7 us -> 0 us
  other arithmetic: 19 us -> 1.5 us
  between operations: 17.7 us -> 0.87 us
    pallas_call x0 -> x3, Pallas kernels: none -> 461 us  [the longest x1 293 us: backward(): pl.pallas_call(functools.partial(backward_kernel, layers, n), out_shape=(...]
    reduce_scatter x6 -> x0, waiting for transfers between devices: 348 us -> none  [step(): lax.psum_scatter(by_w[name], 'dp', scatter_dimension=0, tiled=True)]
    dot_general x15 -> x0, matrix products: 331 us -> none  [the longest x5 123 us: layer(): gate = jnp.dot(a, w['w_gate'], preferred_element_type=jnp.float32)]
    all_gather x6 -> x0, waiting for transfers between devices: 297 us -> none  [fetched(): lax.all_gather(w[number], 'dp', axis=0, tiled=True)]
    psum x1 -> x0, blocking collectives: 38.7 us -> none  [step(): squares = lax.psum(sum((jnp.sum(g * g) for g in gradients)), 'dp')]
    convert_element_type x2 -> x0, other arithmetic: 11 us -> none  [adamw(): return ((w - 0.02 * step).astype(jnp.bfloat16), m, v)]
  transfers between devices with their start and end apart: 12 -> 0, of which waited for: 11 -> 0; matrix products, arithmetic and copies ran while one was open for 23% -> 0% of each run, Pallas kernels for 0% -> 0%
where the time goes in v2:
time: 468 us
  Pallas kernels  461 us (99%)
    pallas_call x1, Pallas kernels, backward(): pl.pallas_call(functools.partial(backward_kernel, layers, n), out_shape=(...  293 us
    pallas_call x1, Pallas kernels, gather(): pl.pallas_call(functools.partial(gather_kernel, layers, n), out_shape=(ja...  155 us
    pallas_call x1, Pallas kernels, update(): pl.pallas_call(functools.partial(update_kernel, count, n), grid=(layers,...  14 us

profile of v2, /device:TPU:96, one launch (start us, length us, event | category | flops | bytes accessed | tf_op | source)
XLA Modules:
  0.0 468.1 jit_solution(18098695283349736639)
XLA Ops:
  0.6 1.8 reshape.38
  2.4 0.0 copy-start
  2.5 0.3 copy.25
  2.7 0.5 stack.7
  3.2 0.5 copy-done
  3.7 0.7 reshape.39
  4.4 0.3 copy.24
  4.7 0.5 stack.8
  5.2 1.5 pad_maximum_fusion.gu_in
  6.7 154.6 %shard_map.178 = (bf16[2,2,4,4,2,16,8192]{6,5,4,3,2,1,0:T(8,128)(2,1)}, bf16[2,4,4,4,128,512]{5,4,3,2,1,0:T(8,128)(2,1)}, bf16[2,1024,512]{2,1,0:T(8,128)(2,1)},...) custom-call(bf16[1024,512]{1,0:T(8,128)(2,1)} %bitcast.18, bf16[2,2,2,16,8192]{4,3,2,1,0:T(8,128)(2,1)} %pad_maximum_fusion.gu_in, ...), custom_call_target="tpu_custom_call" | custom-call | tf_op jit(solution)/shard_map/pallas_call | solution.py:258
  161.3 292.6 %shard_map.179 = (bf16[2,16,2,32,512]{4,3,2,1,0:T(8,128)(2,1)}, bf16[2,4,4,32,512]{4,3,2,1,0:T(8,128)(2,1)}, f32[8,128]{1,0:T(8,128)}) custom-call(bf16[2,1024,512]{2,1,0:T(8,128)(2,1)} %get-tuple-element.17.refs_0_, bf16[2,1024,512]{2,1,0:T(8,128)(2,1)} %get-tuple-element.18.refs_1_, bf16[2,512,1024]{2,1,0:T(8,128)(2,1)} %get-tuple-element.19.refs_2_, ...), custom_call_target="tpu_custom_call" | custom-call | flops 120259084288 | bytes 50331648 | tf_op jit(solution)/shard_map/pallas_call | solution.py:556
  453.9 14.0 %shard_map.180 = (bf16[2,32,8192]{2,1,0:T(8,128)(2,1)}, bf16[2,32,8192]{2,1,0:T(8,128)(2,1)}, bf16[2,512,512]{2,1,0:T(8,128)(2,1)}, f32[2,32,8192]{2,1,0:T(8,128...) custom-call(bf16[2,16,2,32,512]{4,3,2,1,0:T(8,128)(2,1)} %get-tuple-, ...), custom_call_target="tpu_custom_call" | custom-call | tf_op jit(solution)/shard_map/pallas_call | solution.py:615
Async XLA Ops:
  2.4 1.2 copy-start

commit v3 on v2

--- a/solution.py
+++ b/solution.py
@@ -53,30 +53,30 @@
     pl.semaphore_wait(barrier, len(others))
 
 
-def gather_kernel(layers, n, x_in, gu_in, d_in, gu_out, d_out, h_out, a_out, at_out, send, recv, push, pull, own, wsem, total_ref, gub, downb):
-    torus = Torus(n)
+def partner_core():
     rep = lax.axis_index("rep")
-    core = lax.rem(rep, 2)
-    partner = {"rep": rep + 1 - 2 * core}
-    lanes, rows = gu_in.shape[-1] // 2, d_in.shape[-2]
-    tokens, d = x_in.shape
+    return {"rep": rep + 1 - 2 * lax.rem(rep, 2)}
+
+
+def gatherer(torus, units, gu_in, d_in, gu_out, d_out, send, recv, push, pull, own):
+    core, partner = lax.rem(lax.axis_index("rep"), 2), partner_core()
+    lanes, rows = gu_in.shape[-1] // d_in.shape[1], d_in.shape[2] // 2
     parts = {"all": (0, 1), "a": (0, 2), "b": (1, 2)}
 
     def place(k, i, j):
         first, second = torus.step(k, i), torus.step(1 - k, j)
         return (first, second) if k == 0 else (second, first)
 
-    def refs(layer, k, block, part, mine=False, whose=core):
+    def refs(unit, k, block, part, mine=False, whose=core):
+        layer, chunk = lax.div(unit, 2), lax.rem(unit, 2) * 2 + k
         which, of = parts[part]
         wide, high = lanes // of, rows // of
-        cols = pl.ds(k * lanes + which * wide, wide)
-        tall = pl.ds(which * high, high)
+        cols = pl.ds(pl.multiple_of(chunk * lanes + which * wide, wide), wide)
+        tall = pl.ds(pl.multiple_of(whose * rows + which * high, high), high)
         if mine:
-            return gu_in.at[layer, :, whose, :, cols], d_in.at[layer, 2 * whose + k, tall]
+            return gu_in.at[layer, :, whose, :, cols], d_in.at[layer, chunk, tall]
         x, y = block
-        return gu_out.at[layer, :, x, y, whose, :, cols], d_out.at[layer, 2 * whose + k, x, y, tall]
-
-    greet([torus.device(a, b) for a in range(2) for b in SIDES] + [partner])
+        return gu_out.at[layer, :, x, y, whose, :, cols], d_out.at[layer, chunk, x, y, tall]
 
     def owns(layer):
         x, y = torus.at
@@ -85,200 +85,127 @@
             pltpu.make_async_copy(d_in.at[layer], d_out.at[layer, :, x, y], own.at[layer, 1]),
         )
 
-    sent = []
-
-    def message(layer, k, group, kind, i, j):
+    sent = {}
+
+    def message(unit, k, group, kind, i, j):
         axis = k if group == 0 else 1 - k
         part = ("all", "all", "a", "b")[kind]
         target = torus.device(axis, SIDES[kind % 2])
         block = place(k, i, j)
-        there = refs(layer, k, block, part)
-        here = refs(layer, k, block, part, i == 0 and j == 0)
+        there = refs(unit, k, block, part)
+        here = refs(unit, k, block, part, i == 0 and j == 0)
         return [
-            pltpu.make_async_remote_copy(s, t, send.at[layer, k, group, kind, q], recv.at[layer, k, group, kind, q], device_id=target, device_id_type=MESH)
+            pltpu.make_async_remote_copy(s, t, send.at[unit, k, group, kind, q], recv.at[unit, k, group, kind, q], device_id=target, device_id_type=MESH)
             for q, (s, t) in enumerate(zip(here, there, strict=True))
         ]
 
     def out(*which):
         for copy in message(*which):
             copy.start()
-        sent.append((message, which))
+        sent[message, which[1:]] = None
 
     def arrived(*which):
         for copy in message(*which):
             copy.wait_recv()
 
-    def swap(layer, k, number, i, j, theirs=False):
+    def swap(unit, k, number, i, j, theirs=False):
         whose = 1 - core if theirs else core
-        both = refs(layer, k, place(k, i, j), "all", whose=whose)
+        both = refs(unit, k, place(k, i, j), "all", whose=whose)
         return [
-            pltpu.make_async_remote_copy(r, r, push.at[layer, k, number, q], pull.at[layer, k, number, q], device_id=partner, device_id_type=MESH)
+            pltpu.make_async_remote_copy(r, r, push.at[unit, k, number, q], pull.at[unit, k, number, q], device_id=partner, device_id_type=MESH)
             for q, r in enumerate(both)
         ]
 
     def to_partner(*which):
         for copy in swap(*which):
             copy.start()
-        sent.append((swap, which))
+        sent[swap, which[1:]] = None
 
     GROUPS = ((1, 0), (2, -1), (3, 1), (4, 2))
 
-    def first(layer):
+    def first(unit):
         for group in range(2):
             for k in range(2):
                 for kind in range(2):
-                    out(layer, k, group, kind, 0, 0)
-
-    def second(layer):
+                    out(unit, k, group, kind, 0, 0)
+
+    def second(unit):
         for kind, off, group in ((0, -1, 2), (1, 1, 3)):
             for k in range(2):
-                arrived(layer, k, 0, kind, off, 0)
-                out(layer, k, 0, 2 + kind, off, 0)
-                out(layer, k, group, 0, off, 0)
-                out(layer, k, group, 1, off, 0)
-                to_partner(layer, k, kind, off, 0)
-
-    def passed(layer, group, i):
+                arrived(unit, k, 0, kind, off, 0)
+                out(unit, k, 0, 2 + kind, off, 0)
+                out(unit, k, group, 0, off, 0)
+                out(unit, k, group, 1, off, 0)
+                to_partner(unit, k, kind, off, 0)
+
+    def passed(unit, group, i):
         for kind, off in ((0, -1), (1, 1)):
             for k in range(2):
-                arrived(layer, k, group, kind, i, off)
-                out(layer, k, group, 2 + kind, i, off)
-                to_partner(layer, k, 3 * group + kind, i, off)
-
-    def opposite(layer):
+                arrived(unit, k, group, kind, i, off)
+                out(unit, k, group, 2 + kind, i, off)
+                to_partner(unit, k, 3 * group + kind, i, off)
+
+    def opposite(unit):
         for k in range(2):
-            arrived(layer, k, 0, 2, 2, 0)
-            arrived(layer, k, 0, 3, 2, 0)
-            out(layer, k, 4, 0, 2, 0)
-            out(layer, k, 4, 1, 2, 0)
-            to_partner(layer, k, 2, 2, 0)
-
-    def last(layer):
+            arrived(unit, k, 0, 2, 2, 0)
+            arrived(unit, k, 0, 3, 2, 0)
+            out(unit, k, 4, 0, 2, 0)
+            out(unit, k, 4, 1, 2, 0)
+            to_partner(unit, k, 2, 2, 0)
+
+    def last(unit):
         for group, i in GROUPS:
             for k in range(2):
-                arrived(layer, k, group, 2, i, 2)
-                arrived(layer, k, group, 3, i, 2)
-                to_partner(layer, k, 3 * group + 2, i, 2)
-
-    def pulled(layer):
+                arrived(unit, k, group, 2, i, 2)
+                arrived(unit, k, group, 3, i, 2)
+                to_partner(unit, k, 3 * group + 2, i, 2)
+
+    def pulled(unit):
         for k in range(2):
             for number, (i, j) in enumerate([(-1, 0), (1, 0), (2, 0)] + [(i, j) for _, i in GROUPS for j in (-1, 1, 2)]):
-                for copy in swap(layer, k, number, i, j, True):
+                for copy in swap(unit, k, number, i, j, True):
                     copy.wait_recv()
-        for copy in owns(layer):
-            copy.wait()
-
-    def stages(layer):
+
+        @pl.when(lax.rem(unit, 2) == 0)
+        def _():
+            for copy in owns(lax.div(unit, 2)):
+                copy.wait()
+
+    def stages(unit):
         def ahead():
-            if layer + 1 < layers:
-                first(layer + 1)
-            passed(layer, 4, 2)
+            pl.when(unit + 1 < units)(lambda: first(unit + 1))
+            passed(unit, 4, 2)
+
+        def end():
+            last(unit)
+            pulled(unit)
 
         return (
-            lambda: second(layer),
-            lambda: passed(layer, 1, 0),
-            lambda: opposite(layer),
-            lambda: passed(layer, 2, -1),
-            lambda: passed(layer, 3, 1),
+            lambda: second(unit),
+            lambda: passed(unit, 1, 0),
+            lambda: opposite(unit),
+            lambda: passed(unit, 2, -1),
+            lambda: passed(unit, 3, 1),
             ahead,
+            end,
         )
 
-    per = n
-    tiles = d_out.shape[1] * per
-
-    def fetch(layer, s, buf):
-        cols = pl.ds(pl.multiple_of(s * TILE, TILE), TILE)
-        return (
-            pltpu.make_async_copy(gu_out.at[layer, :, :, :, :, :, cols], gub.at[buf], wsem.at[buf, 0]),
-            pltpu.make_async_copy(d_out.at[layer, lax.div(s, per), lax.rem(s, per)], downb.at[buf], wsem.at[buf, 1]),
-        )
-
-    first(0)
-    for layer in range(layers):
-        for copy in owns(layer):
-            copy.start()
-
-    def enter(layer):
-        wide = h_out[layer].astype(F32)
-        wide = wide * scale_of(wide)
-        a_out[layer] = wide.astype(BF)
-        at_out[layer] = wide.T.astype(BF)
-
-    h_out[0] = x_in[...]
-    enter(0)
-    for stage in stages(0):
-        stage()
-    last(0)
-    pulled(0)
-
-    for layer in range(layers - 1):
-        todo = stages(layer + 1)
-        total_ref[...] = jnp.zeros_like(total_ref)
-        for copy in fetch(layer, 0, 0):
-            copy.start()
-
-        def tile_step(s, _, layer=layer, todo=todo):
-            buf = lax.rem(s, 2)
-            for copy in fetch(layer, s, buf):
-                copy.wait()
-
-            @pl.when(s + 1 < tiles)
-            def _():
-                for copy in fetch(layer, s + 1, 1 - buf):
-                    copy.start()
-
-            half = tokens // 2
-            gate_w, up_w = gub[buf, 0].reshape(d, TILE), gub[buf, 1].reshape(d, TILE)
-            for part in range(2):
-                these = pl.ds(part * half, half)
-                gate = dot(a_out[layer, these, :], gate_w)
-                up = dot(a_out[layer, these, :], up_w)
-                act = (gate * jax.nn.sigmoid(gate) * up).astype(BF)
-                total_ref[these, :] += dot(act, downb[buf].reshape(TILE, d))
-
-            for number, stage in enumerate(todo):
-                pl.when(s == 2 * number + 1)(stage)
+    def start():
+        first(0)
+        for layer in range(units // 2):
+            for copy in owns(layer):
+                copy.start()
+
+    def drain():
+        def wait(unit, _):
+            for make, which in sent:
+                for copy in make(unit, *which):
+                    copy.wait_send()
             return 0
 
-        lax.fori_loop(0, tiles, tile_step, 0)
-        h_out[layer + 1] = (h_out[layer].astype(F32) + total_ref[...].astype(BF).astype(F32)).astype(BF)
-        enter(layer + 1)
-        last(layer + 1)
-        pulled(layer + 1)
-
-    for make, which in sent:
-        for copy in make(*which):
-            copy.wait_send()
-
-
-def gather(x, gu, d, n):
-    layers, (tokens, wide) = gu.shape[0], x.shape
-    anywhere, vmem = pl.BlockSpec(memory_space=pl.ANY), pl.BlockSpec(memory_space=pltpu.VMEM)
-    dma = pltpu.SemaphoreType.DMA
-    return pl.pallas_call(
-        functools.partial(gather_kernel, layers, n),
-        out_shape=(
-            jax.ShapeDtypeStruct((layers, 2, n, n) + gu.shape[2:], BF),
-            jax.ShapeDtypeStruct((layers, d.shape[1], n, n) + d.shape[2:], BF),
-            jax.ShapeDtypeStruct((layers, tokens, wide), BF),
-            jax.ShapeDtypeStruct((layers, tokens, wide), BF),
-            jax.ShapeDtypeStruct((layers, wide, tokens), BF),
-        ),
-        in_specs=[vmem] * 3,
-        out_specs=(anywhere, anywhere, vmem, vmem, vmem),
-        scratch_shapes=[
-            dma((layers, 2, 5, 4, 2)),
-            dma((layers, 2, 5, 4, 2)),
-            dma((layers, 2, 15, 2)),
-            dma((layers, 2, 15, 2)),
-            dma((layers, 2)),
-            dma((2, 2)),
-            pltpu.VMEM((tokens, wide), F32),
-            pltpu.VMEM((2, 2, n, n) + gu.shape[2:-1] + (TILE,), BF),
-            pltpu.VMEM((2, n) + d.shape[2:], BF),
-        ],
-        compiler_params=pltpu.CompilerParams(collective_id=0, has_side_effects=True, vmem_limit_bytes=VMEM_LIMIT),
-    )(x, gu, d)
+        lax.fori_loop(0, units, wait, 0)
+
+    return start, stages, drain
 
 
 class Stream:
@@ -365,9 +292,9 @@
 SLOTS = 5 * LAG
 
 
-def backward_kernel(layers, n, *refs):
-    hs_ref, a_ref, at_ref, dy_ref, gu_ref, down_ref, grads_ref, down_grads_ref, squares_ref, by_ref, dag_ref, dau_ref, dg_ref, du_ref, act_ref = refs[:15]
-    gub, downb, wsem, sq_ref, sq_all, sqs, sqr, *stream = refs[15:]
+def step_kernel(layers, n, *refs):
+    x_ref, dy_ref, gu_in, d_in, gu_ref, down_ref, grads_ref, down_grads_ref, squares_ref = refs[:9]
+    hs_ref, a_ref, at_ref, by_ref, dag_ref, dau_ref, dg_ref, du_ref, act_ref, gub, downb, wsem, sq_ref, sq_all, sqs, sqr = refs[9:25]
     tokens, d = dy_ref.shape
     tiles, rows = grads_ref.shape[1], grads_ref.shape[3]
     per = n
@@ -377,7 +304,15 @@
     rounds = layers * chunks * turns
     torus = Torus(n)
 
-    greet([torus.device(a, b) for a in range(2) for b in SIDES] + [torus.device(a, 2) for a in range(2)])
+    greet([torus.device(a, b) for a in range(2) for b in SIDES] + [torus.device(a, 2) for a in range(2)] + [partner_core()])
+
+    start, stages, drain = gatherer(torus, 2 * layers, gu_in, d_in, gu_ref, down_ref, *refs[25:30])
+
+    def enter(layer):
+        wide = hs_ref[layer].astype(F32)
+        wide = wide * scale_of(wide)
+        a_ref[layer] = wide.astype(BF)
+        at_ref[layer] = wide.T.astype(BF)
 
     def store(r, cols, total):
         chunk, turn = lax.div(r, turns), lax.rem(r, turns)
@@ -394,15 +329,58 @@
         wide = total.astype(F32)
         sq_ref[...] += jnp.sum(wide * wide, axis=0)
 
-    sums = Stream(torus, SLOTS, stream, store)
-
-    def fetch(r, buf):
-        layer, tile = layers - 1 - lax.div(r, tiles), lax.rem(r, tiles)
+    sums = Stream(torus, SLOTS, refs[30:], store)
+
+    def fetch(layer, tile, buf):
         cols = pl.ds(pl.multiple_of(tile * TILE, TILE), TILE)
         return (
-            pltpu.make_async_copy(gu_ref.at[layer, :, :, cols], gub.at[buf], wsem.at[buf, 0]),
-            pltpu.make_async_copy(down_ref.at[layer, cols], downb.at[buf], wsem.at[buf, 1]),
+            pltpu.make_async_copy(gu_ref.at[layer, :, :, :, :, :, cols], gub.at[buf], wsem.at[buf, 0]),
+            pltpu.make_async_copy(down_ref.at[layer, lax.div(tile, per), lax.rem(tile, per)], downb.at[buf], wsem.at[buf, 1]),
         )
+
+    def begin(copies):
+        for copy in copies:
+            copy.start()
+
+    def weights(buf):
+        return gub[buf, 0].reshape(d, TILE), gub[buf, 1].reshape(d, TILE), downb[buf].reshape(TILE, d)
+
+    def forward(layer):
+        half, span = tokens // 2, tiles // 2
+        dag_ref[...] = jnp.zeros_like(dag_ref)
+        if layer > 0:
+            begin(fetch(layer, 0, 0))
+
+        def tile_step(i, _):
+            s = i - span
+            buf = lax.rem(i, 2)
+
+            @pl.when(s >= 0)
+            def _():
+                for copy in fetch(layer, s, buf):
+                    copy.wait()
+
+            @pl.when((s + 1 >= 0) & (s + 1 < tiles))
+            def _():
+                begin(fetch(layer, s + 1, 1 - buf))
+
+            @pl.when(s >= 0)
+            def _():
+                gate_w, up_w, down_w = weights(buf)
+                for part in range(2):
+                    these = pl.ds(part * half, half)
+                    gate = dot(a_ref[layer, these, :], gate_w)
+                    up = dot(a_ref[layer, these, :], up_w)
+                    act = (gate * jax.nn.sigmoid(gate) * up).astype(BF)
+                    dag_ref[these, :] += dot(act, down_w)
+
+            for number, stage in enumerate(stages(2 * layer + lax.div(i, span))):
+                pl.when(lax.rem(i, span) == number)(stage)
+            return 0
+
+        lax.fori_loop(span if layer > 0 else 0, span + tiles, tile_step, 0)
+        hs_ref[layer + 1] = (hs_ref[layer].astype(F32) + dag_ref[...].astype(BF).astype(F32)).astype(BF)
+        enter(layer + 1)
 
     def norm_back(layer):
         def block(i, _):
@@ -420,7 +398,7 @@
     def compute(r, layer):
         buf, t = lax.rem(r, 2), lax.rem(r, per)
         first = lax.div(r, per) * turns
-        gate_w, up_w, down_w = gub[buf, 0], gub[buf, 1], downb[buf]
+        gate_w, up_w, down_w = weights(buf)
         half = tokens // 2
         for part in range(2):
             these = pl.ds(part * half, half)
@@ -480,8 +458,12 @@
 
     sq_ref[...] = jnp.zeros_like(sq_ref)
     by_ref[...] = dy_ref[...]
-    for copy in fetch(0, 0):
-        copy.start()
+    start()
+    hs_ref[0] = x_ref[...]
+    enter(0)
+    for layer in range(layers - 1):
+        forward(layer)
+    begin(fetch(layers - 1, 0, 0))
 
     def tile_step(r, _):
         t, first = lax.rem(r, per), lax.div(r, per) * turns
@@ -489,13 +471,12 @@
         @pl.when(r < total_tiles)
         def _():
             layer = layers - 1 - lax.div(r, tiles)
-            for copy in fetch(r, lax.rem(r, 2)):
+            for copy in fetch(layer, lax.rem(r, tiles), lax.rem(r, 2)):
                 copy.wait()
 
             @pl.when(r + 1 < total_tiles)
             def _():
-                for copy in fetch(r + 1, 1 - lax.rem(r, 2)):
-                    copy.start()
+                begin(fetch(layers - 1 - lax.div(r + 1, tiles), lax.rem(r + 1, tiles), 1 - lax.rem(r, 2)))
 
             @pl.when(lax.rem(r, tiles) == 0)
             def _():
@@ -508,11 +489,15 @@
 
             compute(r, layer)
 
+        for number, stage in enumerate(stages(2 * layers - 1)):
+            pl.when(r == number)(stage)
+
         more = 1 + pairs * lax.div(t + 1, per) + (4 * LAG - 1) * lax.div(r, total_tiles)
         lax.fori_loop(first + t, first + t + more, turn, 0)
         return 0
 
     lax.fori_loop(0, total_tiles + 1, tile_step, 0)
+    drain()
 
     mine = jnp.sum(sq_ref[...], axis=0, keepdims=True)
     sq_all[0, 0] = jnp.broadcast_to(mine, sq_all.shape[2:])
@@ -534,8 +519,8 @@
             squares_ref[...] = total
 
 
-def backward(hs, normed, turned, dy, gu, down, n):
-    layers, (tokens, d), ff = hs.shape[0], dy.shape, down.shape[1]
+def gradients(x, dy, gu, down, n):
+    layers, chunks, (tokens, d), ff = gu.shape[0], down.shape[1], x.shape, gu.shape[-1]
     rows, quarter, tiles = d // (n * n), TILE // 4, ff // TILE
     vmem, anywhere = pl.BlockSpec(memory_space=pltpu.VMEM), pl.BlockSpec(memory_space=pl.ANY)
     dma = pltpu.SemaphoreType.DMA
@@ -554,33 +539,43 @@
     ]
 
     return pl.pallas_call(
-        functools.partial(backward_kernel, layers, n),
+        functools.partial(step_kernel, layers, n),
         out_shape=(
+            jax.ShapeDtypeStruct((layers, 2, n, n) + gu.shape[2:], BF),
+            jax.ShapeDtypeStruct((layers, chunks, n, n) + down.shape[2:], BF),
             jax.ShapeDtypeStruct((layers, tiles, 2, rows, TILE), BF),
-            jax.ShapeDtypeStruct((layers, tiles // n, LANES // rows, rows, d), BF),
+            jax.ShapeDtypeStruct((layers, chunks, LANES // rows, rows, d), BF),
             jax.ShapeDtypeStruct((8, LANES), F32),
         ),
-        in_specs=[vmem] * 4 + [anywhere] * 2,
-        out_specs=(vmem, vmem, vmem),
+        in_specs=[vmem] * 4,
+        out_specs=(anywhere, anywhere, vmem, vmem, vmem),
         scratch_shapes=[
+            pltpu.VMEM((layers, tokens, d), BF),
+            pltpu.VMEM((layers, tokens, d), BF),
+            pltpu.VMEM((layers, d, tokens), BF),
             pltpu.VMEM((tokens, d), BF),
             pltpu.VMEM((tokens, d), F32),
             pltpu.VMEM((tokens, d), F32),
             pltpu.VMEM((tokens, TILE), BF),
             pltpu.VMEM((tokens, TILE), BF),
             pltpu.VMEM((tokens, TILE), BF),
-            pltpu.VMEM((2, 2, d, TILE), BF),
-            pltpu.VMEM((2, TILE, d), BF),
+            pltpu.VMEM((2, 2, n, n) + gu.shape[2:-1] + (TILE,), BF),
+            pltpu.VMEM((2, n) + down.shape[2:], BF),
             dma((2, 2)),
             pltpu.VMEM((rows, quarter), F32),
             pltpu.VMEM((2, n, 8, LANES), F32),
             dma((2, n - 1)),
             dma((2, n - 1)),
+            dma((2 * layers, 2, 5, 4, 2)),
+            dma((2 * layers, 2, 5, 4, 2)),
+            dma((2 * layers, 2, 15, 2)),
+            dma((2 * layers, 2, 15, 2)),
+            dma((layers, 2)),
         ]
         + stream,
-        compiler_params=pltpu.CompilerParams(collective_id=1, has_side_effects=True, vmem_limit_bytes=VMEM_LIMIT),
-        cost_estimate=pl.CostEstimate(flops=28 * tokens * d * ff, bytes_accessed=12 * d * ff, transcendentals=2 * tokens * ff),
-    )(hs, normed, turned, dy, gu, down)
+        compiler_params=pltpu.CompilerParams(collective_id=0, has_side_effects=True, vmem_limit_bytes=VMEM_LIMIT),
+        cost_estimate=pl.CostEstimate(flops=34 * tokens * d * ff, bytes_accessed=18 * d * ff, transcendentals=3 * tokens * ff),
+    )(x, dy, gu, down)
 
 
 def update_kernel(count, n, grads_ref, down_grads_ref, squares_ref, *refs):
@@ -639,9 +634,8 @@
         tall = ff // group
         chunks = tall // LANES
         gu = jnp.stack([w.reshape(layers, rows, group, chunks, LANES).swapaxes(2, 3).reshape(layers, rows, ff) for w in weights[:2]], axis=1)
-        gu, down, *states = gather(x[0], gu.reshape(layers, 2, 2, rows // 2, ff), weights[2].reshape(layers, chunks, LANES, d), n)
-        gu, down = gu.reshape(layers, 2, d, ff), down.reshape(layers, ff, d)
-        grads, down_grads, squares = backward(*states, dy[0], gu, down, n)
+        gu, down = gu.reshape(layers, 2, 2, rows // 2, ff), weights[2].reshape(layers, chunks, LANES, d)
+        _, _, grads, down_grads, squares = gradients(x[0], dy[0], gu, down, n)
         return update(grads, down_grads, squares, weights, m, v, n, group * sum(w.size for w in weights))
 
     states, cut = P(("rep", "dp"), None, None), P(None, "dp", None)

time: 468 us -> 467 us (level)
    pallas_call x2 -> x1, Pallas kernels: 447 us -> 446 us  [gradients(): pl.pallas_call(functools.partial(step_kernel, layers, n), out_shape=(jax....]
where the time goes in v3:
time: 467 us; the launch traced here: 466 us
  Pallas kernels  460 us (99%)
    pallas_call x1, Pallas kernels, gradients(): pl.pallas_call(functools.partial(step_kernel, layers, n), out_shape=(jax....  446 us
    pallas_call x1, Pallas kernels, update(): pl.pallas_call(functools.partial(update_kernel, count, n), grid=(layers,...  14 us

profile of v3, /device:TPU:96, one launch (start us, length us, event | category | flops | bytes accessed | tf_op | source)
XLA Modules:
  0.0 466.4 jit_solution(5067479542445884548)
XLA Ops:
  0.6 1.8 reshape.32
  2.4 0.0 copy-start
  2.5 0.3 copy.25
  2.7 0.5 stack.7
  3.2 0.5 copy-done
  3.7 0.7 reshape.33
  4.4 0.3 copy.24
  4.7 0.5 stack.8
  5.2 1.5 pad_maximum_fusion.refs_2_
  6.7 445.5 %shard_map.178 = (bf16[2,2,4,4,2,16,8192]{6,5,4,3,2,1,0:T(8,128)(2,1)}, bf16[2,4,4,4,128,512]{5,4,3,2,1,0:T(8,128)(2,1)}, bf16[2,16,2,32,512]{4,3,2,1,0:T(8,128)...) custom-call(bf16[1024,512]{1,0:T(8,128)(2,1)} %bitcast.16, bf16[1024,512]{1,0:T(8,128)(2,1)} %bitcast.17, ...), custom_call_target="tpu_custom_call" | custom-call | flops 146028888064 | bytes 75497472 | tf_op jit(solution)/shard_map/pallas_call | solution.py:541
  452.2 14.0 %shard_map.179 = (bf16[2,32,8192]{2,1,0:T(8,128)(2,1)}, bf16[2,32,8192]{2,1,0:T(8,128)(2,1)}, bf16[2,512,512]{2,1,0:T(8,128)(2,1)}, f32[2,32,8192]{2,1,0:T(8,128...) custom-call(bf16[2,16,2,32,512]{4,3,2,1,0:T(8,128)(2,1)} %get-tuple-, ...), custom_call_target="tpu_custom_call" | custom-call | tf_op jit(solution)/shard_map/pallas_call | solution.py:610
Async XLA Ops:
  2.4 1.2 copy-start

commit v4 on v3

--- a/solution.py
+++ b/solution.py
@@ -468,6 +468,9 @@
     def tile_step(r, _):
         t, first = lax.rem(r, per), lax.div(r, per) * turns
 
+        for number, stage in enumerate(stages(2 * layers - 1)):
+            pl.when(r == number // 2)(stage)
+
         @pl.when(r < total_tiles)
         def _():
             layer = layers - 1 - lax.div(r, tiles)
@@ -488,9 +491,6 @@
                 dau_ref[...] = jnp.zeros_like(dau_ref)
 
             compute(r, layer)
-
-        for number, stage in enumerate(stages(2 * layers - 1)):
-            pl.when(r == number)(stage)
 
         more = 1 + pairs * lax.div(t + 1, per) + (4 * LAG - 1) * lax.div(r, total_tiles)
         lax.fori_loop(first + t, first + t + more, turn, 0)

time: 467 us -> 466 us (level)
  no operation moved by 1% of the time
where the time goes in v4:
time: 466 us
  Pallas kernels  459 us (98%)
    pallas_call x1, Pallas kernels, gradients(): pl.pallas_call(functools.partial(step_kernel, layers, n), out_shape=(jax....  445 us
    pallas_call x1, Pallas kernels, update(): pl.pallas_call(functools.partial(update_kernel, count, n), grid=(layers,...  14 us

profile of v4, /device:TPU:96, one launch (start us, length us, event | category | flops | bytes accessed | tf_op | source)
XLA Modules:
  0.0 465.8 jit_solution(3696618453504746061)
XLA Ops:
  0.6 1.8 reshape.32
  2.4 0.0 copy-start
  2.5 0.3 copy.25
  2.7 0.5 stack.7
  3.2 0.5 copy-done
  3.7 0.7 reshape.33
  4.4 0.3 copy.24
  4.7 0.5 stack.8
  5.2 1.5 pad_maximum_fusion.refs_2_
  6.7 444.9 %shard_map.178 = (bf16[2,2,4,4,2,16,8192]{6,5,4,3,2,1,0:T(8,128)(2,1)}, bf16[2,4,4,4,128,512]{5,4,3,2,1,0:T(8,128)(2,1)}, bf16[2,16,2,32,512]{4,3,2,1,0:T(8,128)...) custom-call(bf16[1024,512]{1,0:T(8,128)(2,1)} %bitcast.16, bf16[1024,512]{1,0:T(8,128)(2,1)} %bitcast.17, ...), custom_call_target="tpu_custom_call" | custom-call | flops 146028888064 | bytes 75497472 | tf_op jit(solution)/shard_map/pallas_call | solution.py:541
  451.6 14.0 %shard_map.179 = (bf16[2,32,8192]{2,1,0:T(8,128)(2,1)}, bf16[2,32,8192]{2,1,0:T(8,128)(2,1)}, bf16[2,512,512]{2,1,0:T(8,128)(2,1)}, f32[2,32,8192]{2,1,0:T(8,128...) custom-call(bf16[2,16,2,32,512]{4,3,2,1,0:T(8,128)(2,1)} %get-tuple-, ...), custom_call_target="tpu_custom_call" | custom-call | tf_op jit(solution)/shard_map/pallas_call | solution.py:610
Async XLA Ops:
  2.4 1.2 copy-start
